TPU v7x, 256 devices: a whole 4x4x8 slice. The times are simulated.
256 devices in a mesh: lat: 128 (over x, z, y), lev: 2 (over core).
Axes of the slice: x: 4, y: 4, z: 8, core: 2. Of those that a mesh axis runs over, the one named last changes fastest.
Arguments:
- fields: float32 [1280, 3, 16, 2560], P('lat', None, 'lev'), may hold values from 0.1 to 5
- lat_fraction: float32 [1280], P('lat'), may hold values from 0 to 1
- lon_fraction: float32 [1280], P('lat'), may hold values from 0 to 1
- lon_shift: int32 [1280], P('lat'), may hold values from 0 to 2559
- departure_row: int32 [1280], P('lat'), may hold values from 1 to 1277, as said below
- extents: int32 [128, 2], P('lat'), may hold values from 1 to 4
Outputs:
- advected: float32 [1280, 3, 16, 2560], P('lat', None, 'lev')
Inputs may be any that keep to these rules, and one draw needn't show every extreme that they name: departure_row[r] lies within 39 rows of r.
All inputs are finite; a program needn't handle non-finite values.
Results may differ from a plain program's by a relative error of at most 0.0003.
Values sent between devices are 32-bit elements; how exact they have to be, the bound alone decides.
A program may use at most 128 MiB of HBM per device.

v0:
```python
import math

import jax
import jax.numpy as jnp
from jax import lax
from jax.sharding import Mesh
from jax.sharding import PartitionSpec as P

REACH = 4
LAT = ("lat_0", "lat_1", "lat_2")
LAT_LEV = ("lat_0", "lat_1", "lat_2", "lev")


def from_behind(block, axis, distance):
    devices = range(lax.axis_size(axis))
    route = [(i - distance, i) for i in devices if i - distance in devices]
    return lax.ppermute(block, axis, route)


def one_axis_at_a_time(array, axes):
    for axis in axes:
        array = lax.psum(array, axis)
    return array


def cubic_weights(fraction):
    return jnp.stack(
        [
            -fraction * (fraction - 1.0) * (fraction - 2.0) / 6.0,
            (fraction + 1.0) * (fraction - 1.0) * (fraction - 2.0) / 2.0,
            -(fraction + 1.0) * fraction * (fraction - 2.0) / 2.0,
            (fraction + 1.0) * fraction * (fraction - 1.0) / 6.0,
        ]
    )


def along_lon(column, lon_w, shift_value):
    lon_count = column.shape[-1]
    doubled = jnp.concatenate([column, column], axis=-1)
    result = jnp.zeros_like(column)
    for offset in range(4):
        first = (shift_value + offset - 1) % lon_count
        result = result + lon_w[offset] * lax.dynamic_slice_in_dim(doubled, first, lon_count, 2)
    return result


def per_device(fields, lat_fraction, lon_fraction, lon_shift, departure_row, extents):
    row_count = fields.shape[0]
    band_index = lax.axis_index(LAT)
    total_rows = lax.axis_size(LAT) * row_count
    first_row = band_index * row_count
    north_bands = []
    south_bands = []
    band_piece = fields
    for distance in range(REACH):
        band_piece = from_behind(band_piece, LAT, 1)
        north_bands.insert(0, band_piece)
    band_piece = fields
    for distance in range(REACH):
        band_piece = from_behind(band_piece, LAT, -1)
        south_bands.append(band_piece)
    padded = jnp.concatenate(north_bands + [fields] + south_bands, axis=0)
    low_bound = first_row - extents[0, 0] * row_count + 1
    high_bound = first_row + row_count - 3 + extents[0, 1] * row_count
    departure = jnp.clip(jnp.clip(departure_row, low_bound, high_bound), 1, total_rows - 3)
    local_start = departure - 1 - (first_row - REACH * row_count)

    def one_row(inputs):
        start_value, lat_t, lon_t, shift_value = inputs
        row_block = lax.dynamic_slice_in_dim(padded, start_value, 4, 0)
        lat_w = cubic_weights(lat_t)
        column = (
            lat_w[0] * row_block[0]
            + lat_w[1] * row_block[1]
            + lat_w[2] * row_block[2]
            + lat_w[3] * row_block[3]
        )
        return along_lon(column, cubic_weights(lon_t), shift_value)

    moved = lax.map(one_row, (local_start, lat_fraction, lon_fraction, lon_shift))
    row_ids = first_row + jnp.arange(row_count, dtype=jnp.int32)
    area = jnp.cos(math.pi * (row_ids.astype(jnp.float32) + 0.5) / total_rows - math.pi / 2.0)
    local_before = jnp.sum(area[:, None, None, None] * fields, axis=(0, 2, 3))
    local_after = jnp.sum(area[:, None, None, None] * moved, axis=(0, 2, 3))
    mass_before, mass_after = (
        one_axis_at_a_time(local_before, LAT_LEV),
        one_axis_at_a_time(local_after, LAT_LEV),
    )
    return moved * (mass_before / mass_after)[None, :, None, None]


def solution(mesh):
    finer = Mesh(
        mesh.devices.reshape(4, 8, 4, mesh.shape["lev"]), ("lat_0", "lat_1", "lat_2", "lev")
    )
    placed = (P(LAT, None, "lev", None), P(LAT), P(LAT), P(LAT), P(LAT), P(LAT, None))
    return jax.shard_map(
        per_device,
        mesh=finer,
        in_specs=placed,
        out_specs=P(LAT, None, "lev", None),
        check_vma=False,
    )
```

profile of v0, /device:TPU:1, one launch (start us, length us, event | category | flops | bytes accessed | tf_op | source)
XLA Modules:
  0.0 472.4 jit_solution(14239120991809122161)
XLA Ops:
  0.0 4.2 collective-permute-start
  5.5 50.9 %collective-permute-done = f32[10,3,8,2560]{3,2,1,0:T(8,128)S(1)} collective-permute-done((f32[10,3,8,2560]{3,2,1,0:T(8,128)}, f32[10,3,8,2560]{3,2,1,0:T(8,128)S(1)}, u32[]{:S(2)}, u32[]{:S(2)}) %collective-permute-start) | collective-permute-done | bytes 2457632 | tf_op jit(solution)/shard_map/ppermute | solution.py:17
  56.4 4.1 collective-permute-start.1
  61.8 49.7 %collective-permute-done.1 = f32[10,3,8,2560]{3,2,1,0:T(8,128)S(1)} collective-permute-done((f32[10,3,8,2560]{3,2,1,0:T(8,128)S(1)}, f32[10,3,8,2560]{3,2,1,0:T(8,128)S(1)}, u32[]{:S(2)}, u32[]{:S(2)}) %collective-permute-start.1) | collective-permute-done | bytes 2457632 | tf_op jit(solution)/shard_map/ppermute | solution.py:17
  111.5 5.6 %collective-permute-start.2 = (f32[10,3,8,2560]{3,2,1,0:T(8,128)S(1)}, f32[10,3,8,2560]{3,2,1,0:T(8,128)}, u32[]{:S(2)}, u32[]{:S(2)}) collective-permute-start(f32[10,3,8,2560]{3,2,1,0:T(8,128)S(1)} %collective-permute-done.1), channel_id=1, source_target_pairs={{0,2},{2,4},{4,6},{6,8},{8,10},{10,12},{12,14},{14,16},{16,18},{18... | collective-permute-start | bytes 7372808 | tf_op jit(solution)/shard_map/ppermute | solution.py:17
  118.4 47.7 %collective-permute-done.2 = f32[10,3,8,2560]{3,2,1,0:T(8,128)} collective-permute-done((f32[10,3,8,2560]{3,2,1,0:T(8,128)S(1)}, f32[10,3,8,2560]{3,2,1,0:T(8,128)}, u32[]{:S(2)}, u32[]{:S(2)}) %collective-permute-start.2) | collective-permute-done | bytes 2457632 | tf_op jit(solution)/shard_map/ppermute | solution.py:17
  166.1 5.7 %collective-permute-start.3 = (f32[10,3,8,2560]{3,2,1,0:T(8,128)}, f32[10,3,8,2560]{3,2,1,0:T(8,128)}, u32[]{:S(2)}, u32[]{:S(2)}) collective-permute-start(f32[10,3,8,2560]{3,2,1,0:T(8,128)} %collective-permute-done.2), channel_id=1, source_target_pairs={{0,2},{2,4},{4,6},{6,8},{8,10},{10,12},{12,14},{14,16},{16,18},{18... | collective-permute-start | bytes 7372808 | tf_op jit(solution)/shard_map/ppermute | solution.py:17
  171.8 1.4 fusion.17
  176.6 43.7 %collective-permute-done.3 = f32[10,3,8,2560]{3,2,1,0:T(8,128)} collective-permute-done((f32[10,3,8,2560]{3,2,1,0:T(8,128)}, f32[10,3,8,2560]{3,2,1,0:T(8,128)}, u32[]{:S(2)}, u32[]{:S(2)}) %collective-permute-start.3) | collective-permute-done | bytes 2457632 | tf_op jit(solution)/shard_map/ppermute | solution.py:17
  220.2 1.9 constant_dynamic-update-slice_fusion.8
  222.1 2.0 constant_dynamic-update-slice_fusion.7
  224.7 1.5 copy-done.5
  226.4 1.5 copy-done
  228.1 1.5 copy-done.3
  229.8 1.9 constant_dynamic-update-slice_fusion.2
  231.7 1.9 constant_dynamic-update-slice_fusion.1
  233.8 7.3 %copy-done.1 = f32[90,3,8,2560]{3,2,1,0:T(8,128)} copy-done((f32[90,3,8,2560]{3,2,1,0:T(8,128)}, f32[90,3,8,2560]{3,2,1,0:T(8,128)S(1)}, u32[]{:S(2)}) %copy-start.1) | copy-done | bytes 22118424
  241.1 167.7 %while.15 = (s32[]{:T(128)}, f32[10,3,8,2560]{3,2,1,0:T(8,128)S(1)}, f32[10]{0:T(128)S(1)}, f32[10]{0:T(128)S(1)}, s32[10]{0:T(128)S(1)}, /*index=5*/f32[90,3,8,...) while((s32[]{:T(128)}, ...), condition=%wide.region_1.2_spmd, body=%wide.region_0.1_spmd.sunk | while | flops 1106001 | bytes 1721515 | solution.py:80
  248.1 1.4 fusion.20
  281.7 1.4 fusion.20
  298.4 1.4 fusion.20
  315.2 1.4 fusion.20
  332.0 1.4 fusion.20
  348.7 1.4 fusion.20
  365.5 1.4 fusion.20
  382.3 1.4 fusion.20
  408.8 2.3 multiply_reduce_fusion
  411.1 29.6 %all-reduce.2 = (f32[3]{0:T(128)S(1)}, f32[3]{0:T(128)S(1)}) all-reduce(f32[3]{0:T(128)S(1)} %get-tuple-element.190, f32[3]{0:T(128)S(1)} %get-tuple-element.189), channel_id=1, replica_groups=mesh['lat_0'=4,'lat_1'=8,'lat_2'=4,'lev'=2] {'lat_0'}, use_global_device_ids=true, to_apply=%region_3.4 | all-reduce | flops 6 | bytes 48 | tf_op jit(solution)/shard_map/psum | solution.py:22
  440.8 10.7 %all-reduce = (f32[3]{0:T(128)S(1)}, f32[3]{0:T(128)S(1)}) all-reduce(f32[3]{0:T(128)S(1)} %get-tuple-element.209, f32[3]{0:T(128)S(1)} %get-tuple-element.210), channel_id=1, replica_groups=mesh['lat_0'=4,'lat_1'=8,'lat_2'=4,'lev'=2] {'lat_1'}, use_global_device_ids=true, to_apply=%region_4.5 | all-reduce | flops 6 | bytes 48 | tf_op jit(solution)/shard_map/psum | solution.py:22
  451.4 6.0 %all-reduce.1 = (f32[3]{0:T(128)S(1)}, f32[3]{0:T(128)S(1)}) all-reduce(f32[3]{0:T(128)S(1)} %get-tuple-element.205, f32[3]{0:T(128)S(1)} %get-tuple-element.206), channel_id=1, replica_groups=mesh['lat_0'=4,'lat_1'=8,'lat_2'=4,'lev'=2] {'lat_2'}, use_global_device_ids=true, to_apply=%region_5.6 | all-reduce | flops 6 | bytes 48 | tf_op jit(solution)/shard_map/psum | solution.py:22
  457.4 13.2 %all-reduce.3 = (f32[3]{0:T(128)S(1)}, f32[3]{0:T(128)S(1)}) all-reduce(f32[3]{0:T(128)S(1)} %get-tuple-element.207, f32[3]{0:T(128)S(1)} %get-tuple-element.208), channel_id=1, replica_groups=mesh['lat_0'=4,'lat_1'=8,'lat_2'=4,'lev'=2] {'lev'}, use_global_device_ids=true, to_apply=%region_6.7 | all-reduce | flops 6 | bytes 48 | tf_op jit(solution)/shard_map/psum | solution.py:22
  470.6 1.8 broadcast_multiply_fusion
  (87 shorter events, 39.7 us)
Async XLA Ops:
  0.0 56.4 %collective-permute-start = (f32[10,3,8,2560]{3,2,1,0:T(8,128)}, f32[10,3,8,2560]{3,2,1,0:T(8,128)S(1)}, u32[]{:S(2)}, u32[]{:S(2)}) collective-permute-start(f32[10,3,8,2560]{3,2,1,0:T(8,128)} %param.8), channel_id=1, source_target_pairs={{0,2},{2,4},{4,6},{6,8},{8,10},{10,12},{12,14},{14,16},{16,18},{18... | collective-permute-start | bytes 7372808 | tf_op jit(solution)/shard_map/ppermute | solution.py:17
  4.2 56.3 %collective-permute-start.4 = (f32[10,3,8,2560]{3,2,1,0:T(8,128)}, f32[10,3,8,2560]{3,2,1,0:T(8,128)S(1)}, u32[]{:S(2)}, u32[]{:S(2)}) collective-permute-start(f32[10,3,8,2560]{3,2,1,0:T(8,128)} %param.8), channel_id=1, source_target_pairs={{2,0},{4,2},{6,4},{8,6},{10,8},{12,10},{14,12},{16,14},{18,16},{20... | collective-permute-start | bytes 7372808 | tf_op jit(solution)/shard_map/ppermute | solution.py:17
  56.4 115.4 %copy-start.4 = (f32[10,3,8,2560]{3,2,1,0:T(8,128)}, f32[10,3,8,2560]{3,2,1,0:T(8,128)S(1)}, u32[]{:S(2)}) copy-start(f32[10,3,8,2560]{3,2,1,0:T(8,128)S(1)} %collective-permute-done) | copy-start | bytes 7372804
  56.4 55.2 %collective-permute-start.1 = (f32[10,3,8,2560]{3,2,1,0:T(8,128)S(1)}, f32[10,3,8,2560]{3,2,1,0:T(8,128)S(1)}, u32[]{:S(2)}, u32[]{:S(2)}) collective-permute-start(f32[10,3,8,2560]{3,2,1,0:T(8,128)S(1)} %collective-permute-done), channel_id=1, source_target_pairs={{0,2},{2,4},{4,6},{6,8},{8,10},{10,12},{12,14},{14,16},{16,18},{18... | collective-permute-start | bytes 7372808 | tf_op jit(solution)/shard_map/ppermute | solution.py:17
  60.5 111.3 %copy-start.2 = (f32[10,3,8,2560]{3,2,1,0:T(8,128)}, f32[10,3,8,2560]{3,2,1,0:T(8,128)S(1)}, u32[]{:S(2)}) copy-start(f32[10,3,8,2560]{3,2,1,0:T(8,128)S(1)} %collective-permute-done.4) | copy-start | bytes 7372804
  60.5 56.6 %collective-permute-start.5 = (f32[10,3,8,2560]{3,2,1,0:T(8,128)S(1)}, f32[10,3,8,2560]{3,2,1,0:T(8,128)}, u32[]{:S(2)}, u32[]{:S(2)}) collective-permute-start(f32[10,3,8,2560]{3,2,1,0:T(8,128)S(1)} %collective-permute-done.4), channel_id=1, source_target_pairs={{2,0},{4,2},{6,4},{8,6},{10,8},{12,10},{14,12},{16,14},{18,16},{20... | collective-permute-start | bytes 7372808 | tf_op jit(solution)/shard_map/ppermute | solution.py:17
  111.5 60.3 %copy-start.6 = (f32[10,3,8,2560]{3,2,1,0:T(8,128)}, f32[10,3,8,2560]{3,2,1,0:T(8,128)S(1)}, u32[]{:S(2)}) copy-start(f32[10,3,8,2560]{3,2,1,0:T(8,128)S(1)} %collective-permute-done.1) | copy-start | bytes 7372804
  111.5 54.6 %collective-permute-start.2 = (f32[10,3,8,2560]{3,2,1,0:T(8,128)S(1)}, f32[10,3,8,2560]{3,2,1,0:T(8,128)}, u32[]{:S(2)}, u32[]{:S(2)}) collective-permute-start(f32[10,3,8,2560]{3,2,1,0:T(8,128)S(1)} %collective-permute-done.1), channel_id=1, source_target_pairs={{0,2},{2,4},{4,6},{6,8},{8,10},{10,12},{12,14},{14,16},{16,18},{18... | collective-permute-start | bytes 7372808 | tf_op jit(solution)/shard_map/ppermute | solution.py:17
  117.1 58.1 %collective-permute-start.6 = (f32[10,3,8,2560]{3,2,1,0:T(8,128)}, f32[10,3,8,2560]{3,2,1,0:T(8,128)}, u32[]{:S(2)}, u32[]{:S(2)}) collective-permute-start(f32[10,3,8,2560]{3,2,1,0:T(8,128)} %collective-permute-done.5), channel_id=1, source_target_pairs={{2,0},{4,2},{6,4},{8,6},{10,8},{12,10},{14,12},{16,14},{18,16},{20... | collective-permute-start | bytes 7372808 | tf_op jit(solution)/shard_map/ppermute | solution.py:17
  166.1 54.1 %collective-permute-start.3 = (f32[10,3,8,2560]{3,2,1,0:T(8,128)}, f32[10,3,8,2560]{3,2,1,0:T(8,128)}, u32[]{:S(2)}, u32[]{:S(2)}) collective-permute-start(f32[10,3,8,2560]{3,2,1,0:T(8,128)} %collective-permute-done.2), channel_id=1, source_target_pairs={{0,2},{2,4},{4,6},{6,8},{8,10},{10,12},{12,14},{14,16},{16,18},{18... | collective-permute-start | bytes 7372808 | tf_op jit(solution)/shard_map/ppermute | solution.py:17
  175.3 58.3 %collective-permute-start.7 = (f32[10,3,8,2560]{3,2,1,0:T(8,128)}, f32[10,3,8,2560]{3,2,1,0:T(8,128)S(1)}, u32[]{:S(2)}, u32[]{:S(2)}) collective-permute-start(f32[10,3,8,2560]{3,2,1,0:T(8,128)} %collective-permute-done.6), channel_id=1, source_target_pairs={{2,0},{4,2},{6,4},{8,6},{10,8},{12,10},{14,12},{16,14},{18,16},{20... | collective-permute-start | bytes 7372808 | tf_op jit(solution)/shard_map/ppermute | solution.py:17
  222.1 2.4 copy-start.7
  224.5 1.7 copy-start.5
  226.2 1.7 copy-start
  227.9 1.7 copy-start.3
  233.5 7.6 %copy-start.8 = (f32[10]{0:T(128)S(1)}, f32[10]{0:T(128)}, u32[]{:S(2)}) copy-start(f32[10]{0:T(128)} %param.10) | copy-start | bytes 124
  233.5 7.6 %copy-start.9 = (f32[10]{0:T(128)S(1)}, f32[10]{0:T(128)}, u32[]{:S(2)}) copy-start(f32[10]{0:T(128)} %param.9) | copy-start | bytes 124
  233.5 7.6 %copy-start.10 = (s32[10]{0:T(128)S(1)}, s32[10]{0:T(128)}, u32[]{:S(2)}) copy-start(s32[10]{0:T(128)} %param.11) | copy-start | bytes 124
  233.8 7.3 %copy-start.1 = (f32[90,3,8,2560]{3,2,1,0:T(8,128)}, f32[90,3,8,2560]{3,2,1,0:T(8,128)S(1)}, u32[]{:S(2)}) copy-start(f32[90,3,8,2560]{3,2,1,0:T(8,128)S(1)} %constant_dynamic-update-slice_fusion) | copy-start | bytes 66355204
where the time goes:
time: 475 us; the launch traced here: 472 us
  waiting for transfers between devices  192 us (40%)
  loops' own time  124 us (26%)
  blocking collectives  59.5 us (13%)
  local copies, waits for them, and re-layouts  45.7 us (10%)
  other arithmetic  24.8 us (5%)
  starting transfers between devices  24.7 us (5%)
    ppermute x8, waiting for transfers between devices, from_behind(): return lax.ppermute(block, axis, route)  192 us
    another operation x1, loops' own time, per_device(): lax.map(one_row, (local_start, lat_fraction, lon_fraction, lon_shift))  124 us
    psum x4, blocking collectives, one_axis_at_a_time(): array = lax.psum(array, axis)  59.5 us
    ppermute x8, starting transfers between devices, from_behind(): return lax.ppermute(block, axis, route)  24.7 us
    dynamic_slice x40, local copies, waits for them, and re-layouts, per_device(): lax.map(one_row, (local_start, lat_fraction, lon_fraction, lon_shift))  23.5 us
    unnamed x30, local copies, waits for them, and re-layouts  20.6 us
    add x10, other arithmetic, one_row(): lat_w[0] * row_block[0] + lat_w[1] * row_block[1] + lat_w[2] * row_block[2]  13.8 us
  transfers between devices with their start and end apart: 8, of which 4 were waited for; matrix products, arithmetic and copies ran while one was open for 2% of the time, Pallas kernels for 0%

commit v1 on v0

v1 whole, which is shorter than its diff:
```python
import functools
import math

import jax
import jax.numpy as jnp
from jax import lax
from jax.experimental import pallas as pl
from jax.experimental.pallas import tpu as pltpu
from jax.sharding import PartitionSpec as P

MESH = pl.DeviceIdType.MESH
NY, NZ, NX = 4, 8, 4
LANES = 128
SPLITS = 2
ROWS_PER_STEP = 2


def cubic_weights(fraction):
    return [
        -fraction * (fraction - 1.0) * (fraction - 2.0) / 6.0,
        (fraction + 1.0) * (fraction - 1.0) * (fraction - 2.0) / 2.0,
        -(fraction + 1.0) * fraction * (fraction - 2.0) / 2.0,
        (fraction + 1.0) * fraction * (fraction - 1.0) / 6.0,
    ]


def advect_kernel(rows, nfields, lon, chunks, itab_ref, ftab_ref, fields_ref, out_ref, ratio_ref, *scratch):
    count = len(chunks)
    scratch = list(scratch)
    rings = [scratch.pop(0) for _ in range(count)]
    send_up = [scratch.pop(0) for _ in range(count)]
    send_down = [scratch.pop(0) for _ in range(count)]
    recv_up = [scratch.pop(0) for _ in range(count)]
    recv_down = [scratch.pop(0) for _ in range(count)]
    (out_buf, sums, itab_far, ftab_far, itab, ftab, mass,
     load_sem, own_send, own_recv, fwd_send, fwd_recv, z_send, z_recv,
     tab_send, tab_recv, tab_local, sum_send, sum_recv, mass_send, mass_recv, out_sem) = scratch

    band = lax.axis_index("lat")
    core = lax.axis_index("lev")
    bands = NX * NZ * NY
    y = lax.rem(band, NY)
    z = lax.rem(lax.div(band, NY), NZ)
    x = lax.div(band, NY * NZ)
    base = band - y
    ring_rows = NY * rows
    first_ring_row = lax.div(band, NY) * ring_rows

    def in_ring(step):
        return base + lax.rem(y + step, NY)

    y_up, y_far, y_down = [lax.rem(y + s, NY) for s in (1, 2, 3)]
    y_mates = [(in_ring(s), core) for s in (1, 2, 3)]
    z_mates = [(x * (NY * NZ) + lax.rem(z + s, NZ) * NY + y, core) for s in range(1, NZ)]
    x_mates = [(lax.rem(x + s, NX) * (NY * NZ) + z * NY + y, core) for s in range(1, NX)]
    c_mates = [(band, 1 - core)]
    up = (lax.rem(band + NY, bands), core)
    down = (lax.rem(band + bands - NY, bands), core)
    partners = y_mates + z_mates + x_mates + c_mates + [up, down]

    loads = [
        pltpu.make_async_copy(
            fields_ref.at[:, f, :, pl.ds(lane, width)], rings[c].at[pl.ds(y * rows, rows)], load_sem.at[c]
        )
        for c, (f, lane, width) in enumerate(chunks)
    ]
    for load in loads:
        load.start()
    tab_own = [
        pltpu.make_async_copy(itab_ref, itab.at[0], tab_local.at[0]),
        pltpu.make_async_copy(ftab_ref, ftab.at[0], tab_local.at[1]),
    ]
    for copy in tab_own:
        copy.start()

    barrier = pltpu.get_barrier_semaphore()
    for partner in partners:
        pl.semaphore_signal(barrier, inc=1, device_id=partner, device_id_type=MESH)
    pl.semaphore_wait(barrier, len(partners))

    def remote(src, dst, send_sem, recv_sem, target):
        return pltpu.make_async_remote_copy(
            src_ref=src, dst_ref=dst, send_sem=send_sem, recv_sem=recv_sem, device_id=target, device_id_type=MESH
        )

    tables = [
        remote(itab_ref, itab_far.at[1], tab_send.at[0], tab_recv.at[0], up),
        remote(itab_ref, itab_far.at[0], tab_send.at[1], tab_recv.at[1], down),
        remote(ftab_ref, ftab_far.at[1], tab_send.at[2], tab_recv.at[2], up),
        remote(ftab_ref, ftab_far.at[0], tab_send.at[3], tab_recv.at[3], down),
    ]
    for copy in tables:
        copy.start()

    half = rows // 2
    owns, forwards, zsends = [], [], []
    for c in range(count):
        mine = rings[c].at[pl.ds(y * rows, rows)]
        owns.append([
            remote(mine, mine, own_send.at[c, 0], own_recv.at[c, 0], y_mates[0]),
            remote(mine, mine, own_send.at[c, 1], own_recv.at[c, 1], y_mates[2]),
        ])
        from_down = rings[c].at[pl.ds(y_down * rows + half, rows - half)]
        from_up = rings[c].at[pl.ds(y_up * rows, half)]
        forwards.append([
            remote(from_down, from_down, fwd_send.at[c, 0], fwd_recv.at[c, 0], y_mates[0]),
            remote(from_up, from_up, fwd_send.at[c, 1], fwd_recv.at[c, 1], y_mates[2]),
        ])
        zsends.append([
            remote(send_up[c], recv_up[c], z_send.at[c, 0], z_recv.at[c, 0], up),
            remote(send_down[c], recv_down[c], z_send.at[c, 1], z_recv.at[c, 1], down),
        ])

    for c in range(2):
        loads[c].wait()
        for copy in owns[c]:
            copy.start()
    for c in range(2, count):
        loads[c].wait()

    def row_sums(r, carry):
        pieces = []
        for f in range(nfields):
            total = None
            for c, (field, lane, width) in enumerate(chunks):
                if field != f:
                    continue
                block = rings[c][y * rows + r]
                for t in range(width // LANES):
                    tile = block[:, t * LANES:(t + 1) * LANES]
                    total = tile if total is None else total + tile
            pieces.append(jnp.sum(total, axis=0, keepdims=True))
        pieces.append(jnp.zeros((8 - nfields, LANES), jnp.float32))
        sums[y * rows + r] = jnp.concatenate(pieces, axis=0)
        return carry

    lax.fori_loop(0, rows, row_sums, 0)

    for copy in tab_own:
        copy.wait()
    for copy in tables:
        copy.wait_recv()
    tab_in = [
        pltpu.make_async_copy(itab_far.at[0], itab.at[1], tab_local.at[2]),
        pltpu.make_async_copy(itab_far.at[1], itab.at[2], tab_local.at[3]),
        pltpu.make_async_copy(ftab_far.at[0], ftab.at[1], tab_local.at[4]),
        pltpu.make_async_copy(ftab_far.at[1], ftab.at[2], tab_local.at[5]),
    ]
    for copy in tab_in:
        copy.start()
    my_sums = sums.at[pl.ds(y * rows, rows)]
    sum_copies = [remote(my_sums, my_sums, sum_send.at[s], sum_recv.at[s], y_mates[s]) for s in range(NY - 1)]
    for copy in sum_copies:
        copy.start()
    for copy in tab_in:
        copy.wait()

    def taps(t, r):
        first = itab[t, 0, r] - first_ring_row
        out = []
        for a in range(4):
            spot = first + a
            inside = jnp.logical_and(spot >= 0, spot < ring_rows)
            out.append((jnp.clip(spot, 0, ring_rows - 1), jnp.where(inside, ftab[t, a, r], 0.0)))
        return out

    def partial_rows(t, c, dst):
        def one(r, carry):
            acc = None
            for spot, weight in taps(t, r):
                term = weight * rings[c][spot]
                acc = term if acc is None else acc + term
            dst[r] = acc
            return carry

        lax.fori_loop(0, rows, one, 0)

    phases = [x_mates, c_mates, z_mates, y_mates]
    offsets = [0]
    for mates in phases:
        offsets.append(offsets[-1] + len(mates))
    mass_copies = []
    for k, mates in enumerate(phases):
        mass_copies.append([
            remote(mass.at[k], mass.at[len(phases) + 1 + offsets[k] + i], mass_send.at[offsets[k] + i],
                   mass_recv.at[offsets[k] + i], mate)
            for i, mate in enumerate(mates)
        ])

    def mass_step(step):
        if step == 0:
            for copy in sum_copies:
                copy.wait_recv()

            def one(r, carry):
                before, after = carry
                before = before + ftab[0, 9, r] * sums[y * rows + r]
                for t in range(3):
                    moved = None
                    for spot, weight in taps(t, r):
                        term = weight * sums[spot]
                        moved = term if moved is None else moved + term
                    after = after + ftab[t, 4, r] * moved
                return before, after

            zero = jnp.zeros((8, LANES), jnp.float32)
            before, after = lax.fori_loop(0, rows, one, (zero, zero))
        elif step <= len(phases):
            k = step - 1
            before, after = mass[k, 0:8], mass[k, 8:16]
            for i, copy in enumerate(mass_copies[k]):
                copy.wait_recv()
                slot = len(phases) + 1 + offsets[k] + i
                before = before + mass[slot, 0:8]
                after = after + mass[slot, 8:16]
        else:
            return
        if step < len(phases):
            mass[step, 0:8] = before
            mass[step, 8:16] = after
            for copy in mass_copies[step]:
                copy.start()
        else:
            before = jnp.sum(before, axis=1, keepdims=True)
            after = jnp.sum(after, axis=1, keepdims=True)
            ratio_ref[...] = jnp.broadcast_to(before / after, (8, LANES))

    outs = [pltpu.make_async_copy(out_buf.at[f], out_ref.at[:, f], out_sem.at[f]) for f in range(nfields)]

    def finish(f):
        mine = [c for c, chunk in enumerate(chunks) if chunk[0] == f]
        for c in mine:
            for copy in zsends[c]:
                copy.wait_recv()

        def one(r, carry):
            spots = taps(0, r)
            for c in mine:
                _, lane, width = chunks[c]
                acc = recv_up[c][r] + recv_down[c][r]
                for spot, weight in spots:
                    acc = acc + weight * rings[c][spot]
                out_buf[f, r, :, lane:lane + width] = acc
            return carry

        lax.fori_loop(0, rows, one, 0)
        outs[f].start()

    finished = 0
    for c in range(count):
        for copy in owns[c]:
            copy.wait_recv()
        for copy in forwards[c]:
            copy.start()
        if c + 2 < count:
            for copy in owns[c + 2]:
                copy.start()
        for copy in forwards[c]:
            copy.wait_recv()
        partial_rows(1, c, send_up[c])
        partial_rows(2, c, send_down[c])
        for copy in zsends[c]:
            copy.start()
        mass_step(c)
        if c >= len(phases):
            while finished < nfields and chunks[c][0] > finished:
                finish(finished)
                finished += 1
    for step in range(count, len(phases) + 1):
        mass_step(step)
    while finished < nfields:
        finish(finished)
        finished += 1

    for c in range(count):
        for copy in owns[c] + forwards[c] + zsends[c]:
            copy.wait_send()
    for copy in tables + sum_copies:
        copy.wait_send()
    for group in mass_copies:
        for copy in group:
            copy.wait_send()
    for copy in outs:
        copy.wait()


def turn_kernel(nfields, lon, itab, ftab, ratio_ref, column_ref, out_ref, doubled):
    lane_id = lax.broadcasted_iota(jnp.int32, (8, LANES), 1)
    tiles = lon // LANES
    size = lon + 2 * LANES
    for i in range(ROWS_PER_STEP):
        r = pl.program_id(0) * ROWS_PER_STEP + i
        begin = itab[1, r]
        whole = pl.multiple_of(lax.shift_right_logical(begin, 7) * LANES, LANES)
        rest = jnp.bitwise_and(begin, LANES - 1)
        turn = jnp.bitwise_and(LANES - rest, LANES - 1)
        keep = lane_id < (LANES - rest)
        for f in range(nfields):
            column = column_ref[i, f]
            doubled[:, 0:lon] = column
            doubled[:, lon:2 * lon] = column
            doubled[:, 2 * lon:2 * lon + 2 * LANES] = column[:, :2 * LANES]
            window = doubled[:, pl.ds(whole, size)]
            mixed = ftab[5, r] * window
            for k in range(1, 4):
                mixed = mixed + ftab[5 + k, r] * pltpu.roll(window, size - k, 1)
            mixed = mixed * jnp.broadcast_to(ratio_ref[f:f + 1, 0:1], (8, size))
            turned = [pltpu.roll(mixed[:, t * LANES:(t + 1) * LANES], turn, 1) for t in range(tiles + 1)]
            for t in range(tiles):
                out_ref[i, f, :, t * LANES:(t + 1) * LANES] = jnp.where(keep, turned[t], turned[t + 1])


def per_device(fields, lat_fraction, lon_fraction, lon_shift, departure_row, extents):
    rows, nfields, levels, lon = fields.shape
    bands = NX * NZ * NY
    total_rows = bands * rows
    band = lax.axis_index("lat")
    first_row = band * rows
    low = first_row - extents[0, 0] * rows + 1
    high = first_row + rows - 3 + extents[0, 1] * rows
    start = jnp.clip(jnp.clip(departure_row, low, high), 1, total_rows - 3) - 1
    begin = lax.rem(lon_shift + (lon - 1), lon)
    itab = jnp.pad(jnp.stack([start, begin]), ((0, 6), (0, LANES - rows)))
    lat_w = cubic_weights(lat_fraction)
    lon_w = cubic_weights(lon_fraction)
    row_ids = first_row + jnp.arange(rows, dtype=jnp.int32)
    area = jnp.cos(math.pi * (row_ids.astype(jnp.float32) + 0.5) / total_rows - math.pi / 2.0)
    lon_total = lon_w[0] + lon_w[1] + lon_w[2] + lon_w[3]
    ftab = jnp.pad(jnp.stack(lat_w + [area * lon_total] + lon_w + [area]), ((0, 6), (0, LANES - rows)))

    width = lon // SPLITS
    chunks = [(f, s * width, width) for f in range(nfields) for s in range(SPLITS)]
    count = len(chunks)
    dma = pltpu.SemaphoreType.DMA
    mates = (NX - 1) + 1 + (NZ - 1) + (NY - 1)
    scratch = [pltpu.VMEM((NY * rows, levels, w), jnp.float32) for _, _, w in chunks]
    for _ in range(4):
        scratch += [pltpu.VMEM((rows, levels, w), jnp.float32) for _, _, w in chunks]
    scratch += [
        pltpu.VMEM((nfields, rows, levels, lon), jnp.float32),
        pltpu.VMEM((NY * rows, 8, LANES), jnp.float32),
        pltpu.VMEM((2, 8, LANES), jnp.int32),
        pltpu.VMEM((2, 16, LANES), jnp.float32),
        pltpu.SMEM((3, 8, LANES), jnp.int32),
        pltpu.SMEM((3, 16, LANES), jnp.float32),
        pltpu.VMEM((5 + mates, 16, LANES), jnp.float32),
        dma((count,)), dma((count, 2)), dma((count, 2)), dma((count, 2)), dma((count, 2)), dma((count, 2)), dma((count, 2)),
        dma((4,)), dma((4,)), dma((6,)), dma((NY - 1,)), dma((NY - 1,)), dma((mates,)), dma((mates,)), dma((nfields,)),
    ]
    column, ratio = pl.pallas_call(
        functools.partial(advect_kernel, rows, nfields, lon, chunks),
        out_shape=(
            jax.ShapeDtypeStruct(fields.shape, fields.dtype),
            jax.ShapeDtypeStruct((8, LANES), jnp.float32),
        ),
        in_specs=[
            pl.BlockSpec(memory_space=pltpu.VMEM),
            pl.BlockSpec(memory_space=pltpu.VMEM),
            pl.BlockSpec(memory_space=pl.ANY),
        ],
        out_specs=(pl.BlockSpec(memory_space=pl.ANY), pl.BlockSpec(memory_space=pltpu.VMEM)),
        scratch_shapes=scratch,
        compiler_params=pltpu.CompilerParams(collective_id=0, has_side_effects=True),
    )(itab, ftab, fields)
    block = pl.BlockSpec((ROWS_PER_STEP, nfields, levels, lon), lambda i: (i, 0, 0, 0))
    return pl.pallas_call(
        functools.partial(turn_kernel, nfields, lon),
        grid=(rows // ROWS_PER_STEP,),
        out_shape=jax.ShapeDtypeStruct(fields.shape, fields.dtype),
        in_specs=[
            pl.BlockSpec(memory_space=pltpu.SMEM),
            pl.BlockSpec(memory_space=pltpu.SMEM),
            pl.BlockSpec(memory_space=pltpu.VMEM),
            block,
        ],
        out_specs=block,
        scratch_shapes=[pltpu.VMEM((levels, 2 * lon + 2 * LANES), jnp.float32)],
    )(itab, ftab, ratio, column)


def solution(mesh):
    placed = (P("lat", None, "lev", None), P("lat"), P("lat"), P("lat"), P("lat"), P("lat", None))
    return jax.shard_map(
        per_device,
        mesh=mesh,
        in_specs=placed,
        out_specs=P("lat", None, "lev", None),
        check_vma=False,
    )
```

time: 475 us -> 124 us (0.26)
  waiting for transfers between devices: 192 us -> 0 us
  loops' own time: 124 us -> 0 us
  Pallas kernels: 0 us -> 118 us
  blocking collectives: 59.5 us -> 0 us
  local copies, waits for them, and re-layouts: 45.7 us -> 2.54 us
  starting transfers between devices: 24.7 us -> 0 us
  other arithmetic: 24.8 us -> 1.46 us
    ppermute x8 -> x0, waiting for transfers between devices: 192 us -> none  [from_behind(): return lax.ppermute(block, axis, route)]
    another operation x1 -> x0, loops' own time: 124 us -> none  [per_device(): lax.map(one_row, (local_start, lat_fraction, lon_fraction, lon_shift))]
    pallas_call x0 -> x2, Pallas kernels: none -> 118 us  [the longest x1 111 us: per_device(): pl.pallas_call(functools.partial(advect_kernel, rows, nfields, lon, chunk...]
    psum x4 -> x0, blocking collectives: 59.5 us -> none  [one_axis_at_a_time(): array = lax.psum(array, axis)]
    ppermute x8 -> x0, starting transfers between devices: 24.7 us -> none  [from_behind(): return lax.ppermute(block, axis, route)]
    dynamic_slice x40 -> x0, local copies, waits for them, and re-layouts: 23.5 us -> none  [per_device(): lax.map(one_row, (local_start, lat_fraction, lon_fraction, lon_shift))]
    unnamed x30 -> x0, local copies, waits for them, and re-layouts: 20.6 us -> none
    add x10 -> x0, other arithmetic: 13.8 us -> none  [one_row(): lat_w[0] * row_block[0] + lat_w[1] * row_block[1] + lat_w[2] * row_block[2]]
  transfers between devices with their start and end apart: 8 -> 0, of which waited for: 4 -> 0; matrix products, arithmetic and copies ran while one was open for 2% -> 0% of each run, Pallas kernels for 0% -> 0%
where the time goes in v1:
time: 124 us
  Pallas kernels  118 us (95%)
  local copies, waits for them, and re-layouts  2.54 us (2%)
  other arithmetic  1.46 us (1%)
  between operations  1.28 us (1%)
    pallas_call x1, Pallas kernels, per_device(): pl.pallas_call(functools.partial(advect_kernel, rows, nfields, lon, chunk...  111 us
    pallas_call x1, Pallas kernels, per_device(): pl.pallas_call(functools.partial(turn_kernel, nfields, lon), grid=(rows /...  7.2 us

profile of v1, /device:TPU:1, one launch (start us, length us, event | category | flops | bytes accessed | tf_op | source)
XLA Modules:
  0.0 123.7 jit_solution(5158040251643692547)
XLA Ops:
  0.0 1.3 %fusion.4 = (s32[1,1]{1,0:T(1,128)}, s32[1,1]{1,0:T(1,128)}) fusion(s32[1,2]{1,0:T(1,128)} %param.11), kind=kLoop, calls=%fused_computation.21 | loop fusion | bytes 16 | tf_op jit(solution)/shard_map/slice | solution.py:320
  2.6 0.7 remainder_bitcast_fusion
  3.3 0.6 pad.8.itab_ref.itab
  3.9 0.7 multiply_bitcast_fusion.1
  4.7 0.6 pad.9.ftab_ref.ftab
  5.3 111.2 %shard_map.64 = (f32[10,3,8,2560]{3,2,1,0:T(8,128)}, f32[8,128]{1,0:T(8,128)}) custom-call(s32[8,128]{1,0:T(8,128)} %pad.8.itab_ref.itab, f32[16,128]{1,0:T(8,128)} %pad.9.ftab_ref.ftab, f32[10,3,8,2560]{3,2,1,0:T(8,128)} %fields_ref.1), custom_call_target="tpu_custom_call" | custom-call | tf_op jit(solution)/shard_map/pallas_call | solution.py:350
  116.5 7.2 %shard_map.65 = f32[10,3,8,2560]{3,2,1,0:T(8,128)} custom-call(s32[8,128]{1,0:T(8,128)} %pad.8.itab_ref.itab, f32[16,128]{1,0:T(8,128)} %pad.9.ftab_ref.ftab, f32[8,128]{1,0:T(8,128)} %get-tuple-element.7.ratio_ref, f32[10,3,8,2560]{3,2,1,0:T(8,128)} %get-tuple-element.8.column_ref), custom_call_target="tpu_custom_call" | custom-call | tf_op jit(solution)/shard_map/pallas_call | solution.py:366
  (3 shorter events, 0.1 us)

commit v2 on v1

v2 whole, which is shorter than its diff:
```python
import functools
import math

import jax
import jax.numpy as jnp
from jax import lax
from jax.experimental import pallas as pl
from jax.experimental.pallas import tpu as pltpu
from jax.sharding import PartitionSpec as P

MESH = pl.DeviceIdType.MESH
NY, NZ, NX = 4, 8, 4
LANES = 128
ROWS_PER_STEP = 2
CHUNKS = [('ring', 1, 1, 1, 2), ('pair', 2, 1, 1, 2), ('pair', 0, 1, 1, 2), ('column', 0, 0, 1, 2), ('column', 2, 0, 1, 2), ('column', 1, 0, 1, 2)]
ORDER = [0, 3, 2, 5, 3, 0, 4, 5, 2, 1, 3, 4, 5, 0, 2, 1, 4, 3, 2, 0, 1, 4, 5, 1]
MASS_AT = [6, 9, 12, 15, 18]


def cubic_weights(fraction):
    return [
        -fraction * (fraction - 1.0) * (fraction - 2.0) / 6.0,
        (fraction + 1.0) * (fraction - 1.0) * (fraction - 2.0) / 2.0,
        -(fraction + 1.0) * fraction * (fraction - 2.0) / 2.0,
        (fraction + 1.0) * fraction * (fraction - 1.0) / 6.0,
    ]


def buffers_of(scheme, rows, levels, width):
    half = rows // 2
    counts = {
        "ring": [NY * rows] + [rows] * 4,
        "column": [3 * rows] + [rows] * 3 + [half, rows - half] + [rows] * 2,
        "pair": [2 * rows] + [rows] * 8,
    }[scheme]
    return [pltpu.VMEM((n, levels, width), jnp.float32) for n in counts]


COPIES = {"ring": 6, "column": 6, "pair": 5}


def advect_kernel(rows, nfields, lon, chunks, *refs):
    refs = list(refs)
    lat_ref, lon_ref, departure_ref, extents_ref, fields_ref, out_ref, ratio_ref = refs[:7]
    scratch = refs[7:]
    count = len(chunks)
    bufs = []
    for chunk in chunks:
        n = len(buffers_of(chunk[0], rows, 8, LANES))
        bufs.append(scratch[:n])
        scratch = scratch[n:]
    (out_buf, sums, itab_all, ftab_all, itab, ftab, mass,
     load_sem, bulk_send, bulk_recv, tab_send, tab_recv, tab_local,
     sum_send, sum_recv, mass_send, mass_recv, out_sem) = scratch

    band = lax.axis_index("lat")
    core = lax.axis_index("lev")
    bands = NX * NZ * NY
    y = lax.rem(band, NY)
    z = lax.rem(lax.div(band, NY), NZ)
    x = lax.div(band, NY * NZ)
    base = band - y
    odd = lax.rem(y, 2)
    south = lax.div(y, 2)

    y_up, y_down = lax.rem(y + 1, NY), lax.rem(y + 3, NY)
    y_mates = [(base + lax.rem(y + s, NY), core) for s in (1, 2, 3)]
    z_mates = [(x * (NY * NZ) + lax.rem(z + s, NZ) * NY + y, core) for s in range(1, NZ)]
    x_mates = [(lax.rem(x + s, NX) * (NY * NZ) + z * NY + y, core) for s in range(1, NX)]
    c_mates = [(band, 1 - core)]
    up = (lax.rem(band + NY, bands), core)
    down = (lax.rem(band + bands - NY, bands), core)
    pair = (band + 1 - 2 * odd, core)
    cross = (base + 3 - y, core)
    toward = (lax.rem(band + bands - NY + 2 * NY * south, bands), core)
    diagonal = (lax.rem(base + 3 - y + bands - NY + 2 * NY * south, bands), core)
    partners = y_mates + z_mates + x_mates + c_mates + [up, down, diagonal]

    own_at = {"ring": y * rows, "column": rows, "pair": odd * rows}
    loads = [
        pltpu.make_async_copy(
            fields_ref.at[:, f, :, pl.ds(lane, width)],
            bufs[c][0].at[pl.ds(own_at[scheme], rows)],
            load_sem.at[c],
        )
        for c, (scheme, f, lane, width) in enumerate(chunks)
    ]
    loaded_first = []
    for c in ORDER + list(range(count)):
        if c not in loaded_first:
            loaded_first.append(c)
    for c in loaded_first:
        loads[c].start()

    barrier = pltpu.get_barrier_semaphore()
    for partner in partners:
        pl.semaphore_signal(barrier, inc=1, device_id=partner, device_id_type=MESH)

    first_row = band * rows
    low = first_row - extents_ref[0:1, 0:1] * rows + 1
    high = first_row + rows - 3 + extents_ref[0:1, 1:2] * rows
    start = jnp.minimum(jnp.maximum(departure_ref[...], low), high)
    start = jnp.minimum(jnp.maximum(start, 1), bands * rows - 3) - 1
    lat_w = cubic_weights(lat_ref[...])
    lon_w = cubic_weights(lon_ref[...])
    row_ids = first_row + lax.broadcasted_iota(jnp.int32, (1, rows), 1)
    area = jnp.cos(math.pi * (row_ids.astype(jnp.float32) + 0.5) / (bands * rows) - math.pi / 2.0)
    lon_total = lon_w[0] + lon_w[1] + lon_w[2] + lon_w[3]
    itab_all[0] = jnp.zeros((8, LANES), jnp.int32)
    ftab_all[0] = jnp.zeros((16, LANES), jnp.float32)
    itab_all[0, 0:1, 0:rows] = start
    for k, values in enumerate(lat_w + [area * lon_total] + lon_w + [area]):
        ftab_all[0, k:k + 1, 0:rows] = values

    for load in loads:
        load.wait()

    def row_sums(r, carry):
        pieces = []
        for f in range(nfields):
            total = None
            for c, (scheme, field, lane, width) in enumerate(chunks):
                if field != f:
                    continue
                block = bufs[c][0][own_at[scheme] + r]
                for t in range(width // LANES):
                    tile = block[:, t * LANES:(t + 1) * LANES]
                    total = tile if total is None else total + tile
            pieces.append(jnp.sum(total, axis=0, keepdims=True))
        pieces.append(jnp.zeros((8 - nfields, LANES), jnp.float32))
        sums[y * rows + r] = jnp.concatenate(pieces, axis=0)
        return carry

    lax.fori_loop(0, rows, row_sums, 0)
    pl.semaphore_wait(barrier, len(partners))

    def remote(src, dst, send_sem, recv_sem, target):
        return pltpu.make_async_remote_copy(
            src_ref=src, dst_ref=dst, send_sem=send_sem, recv_sem=recv_sem, device_id=target, device_id_type=MESH
        )

    table_routes = [(2, up), (1, down), (5, y_mates[0]), (4, y_mates[1]), (3, y_mates[2]), (6, diagonal)]
    tables = []
    for i, (slot, target) in enumerate(table_routes):
        for j, ref in enumerate((itab_all, ftab_all)):
            tables.append(remote(ref.at[0], ref.at[slot], tab_send.at[2 * i + j], tab_recv.at[2 * i + j], target))
    for copy in tables:
        copy.start()
    my_sums = sums.at[pl.ds(y * rows, rows)]
    sum_copies = [remote(my_sums, my_sums, sum_send.at[s], sum_recv.at[s], y_mates[s]) for s in range(NY - 1)]

    def ring_spot(row):
        spot = row - base * rows
        return jnp.clip(spot, 0, NY * rows - 1), jnp.logical_and(spot >= 0, spot < NY * rows)

    def pair_spot(row):
        spot = row - (band - odd) * rows
        return jnp.clip(spot, 0, 2 * rows - 1), jnp.logical_and(spot >= 0, spot < 2 * rows)

    def column_spot(row):
        away = row - (band - NY) * rows
        block = (away >= NY * rows).astype(jnp.int32) + (away >= 2 * NY * rows).astype(jnp.int32)
        within = away - block * (NY * rows)
        return block * rows + jnp.clip(within, 0, rows - 1), jnp.logical_and(within >= 0, within < rows)

    def taps(spot_of, t, r):
        first = itab[t, 0, r]
        out = []
        for a in range(4):
            spot, inside = spot_of(first + a)
            out.append((spot, jnp.where(inside, ftab[t, a, r], 0.0)))
        return out

    def weighted(ref, spots):
        acc = None
        for spot, weight in spots:
            term = weight * ref[spot]
            acc = term if acc is None else acc + term
        return acc

    def partial_rows(spot_of, src, jobs):
        def one(r, carry):
            for t, dst, extra in jobs:
                acc = weighted(src, taps(spot_of, t, r))
                dst[r] = acc if extra is None else acc + extra[r]
            return carry

        lax.fori_loop(0, rows, one, 0)

    def add_rows(n, dst, dst_at, extra):
        def one(r, carry):
            dst[dst_at + r] = dst[dst_at + r] + extra[r]
            return carry

        lax.fori_loop(0, n, one, 0)

    ready = []

    def need_tables():
        if ready:
            return
        ready.append(True)
        for copy in tables:
            copy.wait_recv()
        moves = [
            pltpu.make_async_copy(itab_all, itab, tab_local.at[0]),
            pltpu.make_async_copy(ftab_all, ftab, tab_local.at[1]),
        ]
        for copy in moves:
            copy.start()
        for copy in moves:
            copy.wait()

    half = rows // 2
    finals = [None] * count

    def stages_of(c):
        scheme = chunks[c][0]
        b = bufs[c]
        send = [bulk_send.at[c, k] for k in range(COPIES[scheme])]
        recv = [bulk_recv.at[c, k] for k in range(COPIES[scheme])]

        def link(k, src, dst, target):
            return remote(src, dst, send[k], recv[k], target)

        if scheme == "ring":
            ring, send_up, send_down, recv_up, recv_down = b
            mine = ring.at[pl.ds(y * rows, rows)]
            from_down = ring.at[pl.ds(y_down * rows + half, rows - half)]
            from_up = ring.at[pl.ds(y_up * rows, half)]
            copies = [
                link(0, mine, mine, y_mates[0]), link(1, mine, mine, y_mates[2]),
                link(2, from_down, from_down, y_mates[0]), link(3, from_up, from_up, y_mates[2]),
                link(4, send_up, recv_up, up), link(5, send_down, recv_down, down),
            ]

            def stage0():
                copies[0].start()
                copies[1].start()

            def stage1():
                copies[0].wait_recv()
                copies[1].wait_recv()
                copies[2].start()
                copies[3].start()

            def stage2():
                copies[2].wait_recv()
                copies[3].wait_recv()
                need_tables()
                partial_rows(ring_spot, ring, [(1, send_up, None), (2, send_down, None)])
                copies[4].start()
                copies[5].start()

            def stage3():
                copies[4].wait_recv()
                copies[5].wait_recv()
                finals[c] = (ring_spot, ring, [recv_up, recv_down])

        elif scheme == "column":
            column, to_up, to_down, to_far, far_a, far_b, got_a, got_b = b
            mine = column.at[pl.ds(rows, rows)]
            copies = [
                link(0, mine, column.at[pl.ds(0, rows)], up), link(1, mine, column.at[pl.ds(2 * rows, rows)], down),
                link(2, to_far.at[pl.ds(0, half)], far_a, y_mates[0]),
                link(3, to_far.at[pl.ds(half, rows - half)], far_b, y_mates[2]),
                link(4, to_up, got_a, y_mates[0]), link(5, to_down, got_b, y_mates[2]),
            ]

            def stage0():
                copies[0].start()
                copies[1].start()

            def stage1():
                copies[0].wait_recv()
                copies[1].wait_recv()
                need_tables()
                partial_rows(column_spot, column, [(4, to_far, None)])
                copies[2].start()
                copies[3].start()
                partial_rows(column_spot, column, [(3, to_up, None), (5, to_down, None)])

            def stage2():
                copies[2].wait_recv()
                add_rows(half, to_up, 0, far_a)
                copies[4].start()
                copies[3].wait_recv()
                add_rows(rows - half, to_down, half, far_b)
                copies[5].start()

            def stage3():
                copies[4].wait_recv()
                copies[5].wait_recv()
                finals[c] = (column_spot, column, [got_a, got_b])

        else:
            both, to_up, to_down, to_diag, to_cross, from_down, from_up, passed, from_cross = b
            mine = both.at[pl.ds(odd * rows, rows)]
            copies = [
                link(0, mine, mine, pair), link(1, to_up, from_down, up), link(2, to_down, from_up, down),
                link(3, to_diag, passed, toward), link(4, to_cross, from_cross, cross),
            ]

            def stage0():
                copies[0].start()

            def stage1():
                copies[0].wait_recv()
                need_tables()
                partial_rows(pair_spot, both, [(6, to_diag, None)])
                copies[3].start()
                partial_rows(pair_spot, both, [(1, to_up, None), (2, to_down, None)])
                copies[1].start()
                copies[2].start()

            def stage2():
                copies[3].wait_recv()
                partial_rows(pair_spot, both, [(5 - 2 * odd, to_cross, passed)])
                copies[4].start()

            def stage3():
                copies[1].wait_recv()
                copies[2].wait_recv()
                copies[4].wait_recv()
                finals[c] = (pair_spot, both, [from_down, from_up, from_cross])

        return copies, [stage0, stage1, stage2, stage3]

    phases = [x_mates, c_mates, z_mates, y_mates]
    offsets = [0]
    for mates in phases:
        offsets.append(offsets[-1] + len(mates))
    mass_copies = []
    for k, mates in enumerate(phases):
        mass_copies.append([
            remote(mass.at[k], mass.at[len(phases) + offsets[k] + i], mass_send.at[offsets[k] + i],
                   mass_recv.at[offsets[k] + i], mate)
            for i, mate in enumerate(mates)
        ])

    def mass_step(step):
        if step == 0:
            need_tables()
            for copy in sum_copies:
                copy.wait_recv()

            def one(r, carry):
                before, after = carry
                before = before + ftab[0, 9, r] * sums[y * rows + r]
                for t in range(3):
                    after = after + ftab[t, 4, r] * weighted(sums, taps(ring_spot, t, r))
                return before, after

            zero = jnp.zeros((8, LANES), jnp.float32)
            before, after = lax.fori_loop(0, rows, one, (zero, zero))
        else:
            k = step - 1
            before, after = mass[k, 0:8], mass[k, 8:16]
            for i, copy in enumerate(mass_copies[k]):
                copy.wait_recv()
                slot = len(phases) + offsets[k] + i
                before = before + mass[slot, 0:8]
                after = after + mass[slot, 8:16]
        if step < len(phases):
            mass[step, 0:8] = before
            mass[step, 8:16] = after
            for copy in mass_copies[step]:
                copy.start()
        else:
            before = jnp.sum(before, axis=1, keepdims=True)
            after = jnp.sum(after, axis=1, keepdims=True)
            ratio_ref[...] = jnp.broadcast_to(before / after, (8, LANES))

    outs = [pltpu.make_async_copy(out_buf.at[f], out_ref.at[:, f], out_sem.at[f]) for f in range(nfields)]

    def finish(c):
        _, f, lane, width = chunks[c]
        spot_of, src, extras = finals[c]

        def one(r, carry):
            acc = weighted(src, taps(spot_of, 0, r))
            for extra in extras:
                acc = acc + extra[r]
            out_buf[f, r, :, lane:lane + width] = acc
            return carry

        lax.fori_loop(0, rows, one, 0)

    def filter_rows(f):
        def one(r, carry):
            column = out_buf[f, r]
            mixed = ftab[0, 5, r] * column
            for k in range(1, 4):
                mixed = mixed + ftab[0, 5 + k, r] * pltpu.roll(column, lon - k, 1)
            out_buf[f, r] = mixed
            return carry

        lax.fori_loop(0, rows, one, 0)
        outs[f].start()

    every = [stages_of(c) for c in range(count)]
    place = [0] * count
    left = [sum(1 for chunk in chunks if chunk[1] == f) for f in range(nfields)]
    mass_done = 0
    for i, c in enumerate(ORDER):
        every[c][1][place[c]]()
        place[c] += 1
        if i == 1:
            for copy in sum_copies:
                copy.start()
        if place[c] == 4:
            finish(c)
            f = chunks[c][1]
            left[f] -= 1
            if left[f] == 0:
                filter_rows(f)
        while mass_done < len(MASS_AT) and MASS_AT[mass_done] == i:
            mass_step(mass_done)
            mass_done += 1

    for copies, _ in every:
        for copy in copies:
            copy.wait_send()
    for copy in tables + sum_copies:
        copy.wait_send()
    for group in mass_copies:
        for copy in group:
            copy.wait_send()
    for copy in outs:
        copy.wait()


def turn_kernel(nfields, lon, shift_ref, ratio_ref, column_ref, out_ref):
    lane_id = lax.broadcasted_iota(jnp.int32, (8, LANES), 1)
    tiles = lon // LANES
    for i in range(ROWS_PER_STEP):
        r = pl.program_id(0) * ROWS_PER_STEP + i
        begin = shift_ref[r] - 1
        begin = jnp.where(begin < 0, begin + lon, begin)
        whole = lax.shift_right_logical(begin, 7)
        rest = jnp.bitwise_and(begin, LANES - 1)
        turn = jnp.bitwise_and(LANES - rest, LANES - 1)
        keep = lane_id < (LANES - rest)
        spots = []
        for t in range(tiles + 1):
            spot = whole + t
            spot = jnp.where(spot >= tiles, spot - tiles, spot)
            spots.append(pl.multiple_of(spot * LANES, LANES))
        for f in range(nfields):
            ratio = jnp.broadcast_to(ratio_ref[f:f + 1, :], (8, LANES))
            turned = [pltpu.roll(column_ref[i, f, :, pl.ds(spot, LANES)], turn, 1) for spot in spots]
            for t in range(tiles):
                out_ref[i, f, :, t * LANES:(t + 1) * LANES] = jnp.where(keep, turned[t], turned[t + 1]) * ratio


def per_device(fields, lat_fraction, lon_fraction, lon_shift, departure_row, extents):
    rows, nfields, levels, lon = fields.shape
    chunks = [(k, f, lon * lane // parts, lon * width // parts) for k, f, lane, width, parts in CHUNKS]
    count = len(chunks)
    dma = pltpu.SemaphoreType.DMA
    mates = (NX - 1) + 1 + (NZ - 1) + (NY - 1)
    scratch = []
    for scheme, _, _, width in chunks:
        scratch += buffers_of(scheme, rows, levels, width)
    scratch += [
        pltpu.VMEM((nfields, rows, levels, lon), jnp.float32),
        pltpu.VMEM((NY * rows, 8, LANES), jnp.float32),
        pltpu.VMEM((7, 8, LANES), jnp.int32),
        pltpu.VMEM((7, 16, LANES), jnp.float32),
        pltpu.SMEM((7, 8, LANES), jnp.int32),
        pltpu.SMEM((7, 16, LANES), jnp.float32),
        pltpu.VMEM((4 + mates, 16, LANES), jnp.float32),
        dma((count,)), dma((count, 6)), dma((count, 6)), dma((12,)), dma((12,)), dma((2,)),
        dma((NY - 1,)), dma((NY - 1,)), dma((mates,)), dma((mates,)), dma((nfields,)),
    ]
    vmem = pl.BlockSpec(memory_space=pltpu.VMEM)
    column, ratio = pl.pallas_call(
        functools.partial(advect_kernel, rows, nfields, lon, chunks),
        out_shape=(
            jax.ShapeDtypeStruct(fields.shape, fields.dtype),
            jax.ShapeDtypeStruct((8, LANES), jnp.float32),
        ),
        in_specs=[vmem, vmem, vmem, vmem, pl.BlockSpec(memory_space=pl.ANY)],
        out_specs=(pl.BlockSpec(memory_space=pl.ANY), vmem),
        scratch_shapes=scratch,
        compiler_params=pltpu.CompilerParams(collective_id=0, has_side_effects=True),
    )(lat_fraction[None], lon_fraction[None], departure_row[None], extents, fields)
    block = pl.BlockSpec((ROWS_PER_STEP, nfields, levels, lon), lambda i: (i, 0, 0, 0))
    return pl.pallas_call(
        functools.partial(turn_kernel, nfields, lon),
        grid=(rows // ROWS_PER_STEP,),
        out_shape=jax.ShapeDtypeStruct(fields.shape, fields.dtype),
        in_specs=[pl.BlockSpec(memory_space=pltpu.SMEM), vmem, block],
        out_specs=block,
    )(lon_shift, ratio, column)


def solution(mesh):
    placed = (P("lat", None, "lev", None), P("lat"), P("lat"), P("lat"), P("lat"), P("lat", None))
    return jax.shard_map(
        per_device,
        mesh=mesh,
        in_specs=placed,
        out_specs=P("lat", None, "lev", None),
        check_vma=False,
    )
```

time: 124 us -> 118 us (0.952)
  local copies, waits for them, and re-layouts: 2.54 us -> 0 us
  other arithmetic: 1.46 us -> 0 us
  between operations: 1.28 us -> 0.01 us
    pallas_call x1, Pallas kernels: 7.2 us -> 5.19 us  [per_device(): pl.pallas_call(functools.partial(turn_kernel, nfields, lon), grid=(rows /...]
    pallas_call x1, Pallas kernels: 111 us -> 113 us  [per_device(): pl.pallas_call(functools.partial(advect_kernel, rows, nfields, lon, chunk...]
    another operation x3 -> x0, other arithmetic: 1.41 us -> none  [the longest x1 0.72 us: per_device(): jnp.stack(lat_w + [area * lon_total] + lon_w + [area])]
    slice x1 -> x0, local copies, waits for them, and re-layouts: 1.32 us -> none  [per_device(): high = first_row + rows - 3 + extents[0, 1] * rows]
where the time goes in v2:
time: 118 us
  Pallas kernels  118 us (100%)
    pallas_call x1, Pallas kernels, per_device(): pl.pallas_call(functools.partial(advect_kernel, rows, nfields, lon, chunk...  113 us
    pallas_call x1, Pallas kernels, per_device(): pl.pallas_call(functools.partial(turn_kernel, nfields, lon), grid=(rows /...  5.19 us

profile of v2, /device:TPU:1, one launch (start us, length us, event | category | flops | bytes accessed | tf_op | source)
XLA Modules:
  0.0 118.2 jit_solution(8590914478973457558)
XLA Ops:
  0.0 113.0 %shard_map.64 = (f32[10,3,8,2560]{3,2,1,0:T(8,128)}, f32[8,128]{1,0:T(8,128)}) custom-call(f32[1,10]{1,0:T(1,128)} %bitcast.3, f32[1,10]{1,0:T(1,128)} %bitcast.4, s32[1,10]{1,0:T(1,128)} %bitcast.5, s32[1,2]{1,0:T(1,128)} %refs_3_.1, f32[10,3,8,2560]{3,2,1,0:T(8,128)} %refs_4_.1), custom_call_target="tpu_custom_call" | custom-call | tf_op jit(solution)/shard_map/pallas_call | solution.py:477
  113.0 5.2 %shard_map.65 = f32[10,3,8,2560]{3,2,1,0:T(8,128)} custom-call(s32[10]{0:T(128)} %shift_ref.1, f32[8,128]{1,0:T(8,128)} %get-tuple-element.7.ratio_ref, f32[10,3,8,2560]{3,2,1,0:T(8,128)} %get-tuple-element.8.column_ref), custom_call_target="tpu_custom_call" | custom-call | tf_op jit(solution)/shard_map/pallas_call | solution.py:489

commit v3 on v2

--- a/solution.py
+++ b/solution.py
@@ -14,7 +14,7 @@
 ROWS_PER_STEP = 2
 CHUNKS = [('ring', 1, 1, 1, 2), ('pair', 2, 1, 1, 2), ('pair', 0, 1, 1, 2), ('column', 0, 0, 1, 2), ('column', 2, 0, 1, 2), ('column', 1, 0, 1, 2)]
 ORDER = [0, 3, 2, 5, 3, 0, 4, 5, 2, 1, 3, 4, 5, 0, 2, 1, 4, 3, 2, 0, 1, 4, 5, 1]
-MASS_AT = [6, 9, 12, 15, 18]
+MASS_AT = [2, 8, 15, 16, 23]
 
 
 def cubic_weights(fraction):
@@ -148,6 +148,8 @@
         copy.start()
     my_sums = sums.at[pl.ds(y * rows, rows)]
     sum_copies = [remote(my_sums, my_sums, sum_send.at[s], sum_recv.at[s], y_mates[s]) for s in range(NY - 1)]
+    for copy in sum_copies:
+        copy.start()
 
     def ring_spot(row):
         spot = row - base * rows
@@ -326,7 +328,7 @@
 
         return copies, [stage0, stage1, stage2, stage3]
 
-    phases = [x_mates, c_mates, z_mates, y_mates]
+    phases = [y_mates, z_mates, c_mates, x_mates]
     offsets = [0]
     for mates in phases:
         offsets.append(offsets[-1] + len(mates))
@@ -353,23 +355,20 @@
 
             zero = jnp.zeros((8, LANES), jnp.float32)
             before, after = lax.fori_loop(0, rows, one, (zero, zero))
+            total = jnp.concatenate([before[0:4], after[0:4]], axis=0)
         else:
             k = step - 1
-            before, after = mass[k, 0:8], mass[k, 8:16]
+            total = mass[k]
             for i, copy in enumerate(mass_copies[k]):
                 copy.wait_recv()
-                slot = len(phases) + offsets[k] + i
-                before = before + mass[slot, 0:8]
-                after = after + mass[slot, 8:16]
+                total = total + mass[len(phases) + offsets[k] + i]
         if step < len(phases):
-            mass[step, 0:8] = before
-            mass[step, 8:16] = after
+            mass[step] = total
             for copy in mass_copies[step]:
                 copy.start()
         else:
-            before = jnp.sum(before, axis=1, keepdims=True)
-            after = jnp.sum(after, axis=1, keepdims=True)
-            ratio_ref[...] = jnp.broadcast_to(before / after, (8, LANES))
+            total = jnp.sum(total, axis=1, keepdims=True)
+            ratio_ref[0:4] = jnp.broadcast_to(total[0:4] / total[4:8], (4, LANES))
 
     outs = [pltpu.make_async_copy(out_buf.at[f], out_ref.at[:, f], out_sem.at[f]) for f in range(nfields)]
 
@@ -405,9 +404,6 @@
     for i, c in enumerate(ORDER):
         every[c][1][place[c]]()
         place[c] += 1
-        if i == 1:
-            for copy in sum_copies:
-                copy.start()
         if place[c] == 4:
             finish(c)
             f = chunks[c][1]
@@ -469,7 +465,7 @@
         pltpu.VMEM((7, 16, LANES), jnp.float32),
         pltpu.SMEM((7, 8, LANES), jnp.int32),
         pltpu.SMEM((7, 16, LANES), jnp.float32),
-        pltpu.VMEM((4 + mates, 16, LANES), jnp.float32),
+        pltpu.VMEM((4 + mates, 8, LANES), jnp.float32),
         dma((count,)), dma((count, 6)), dma((count, 6)), dma((12,)), dma((12,)), dma((2,)),
         dma((NY - 1,)), dma((NY - 1,)), dma((mates,)), dma((mates,)), dma((nfields,)),
     ]
@@ -478,7 +474,7 @@
         functools.partial(advect_kernel, rows, nfields, lon, chunks),
         out_shape=(
             jax.ShapeDtypeStruct(fields.shape, fields.dtype),
-            jax.ShapeDtypeStruct((8, LANES), jnp.float32),
+            jax.ShapeDtypeStruct((4, LANES), jnp.float32),
         ),
         in_specs=[vmem, vmem, vmem, vmem, pl.BlockSpec(memory_space=pl.ANY)],
         out_specs=(pl.BlockSpec(memory_space=pl.ANY), vmem),

time: 118 us -> 96.8 us (0.82)
  Pallas kernels: 118 us -> 96.2 us
    pallas_call x1, Pallas kernels: 113 us -> 91 us  [per_device(): pl.pallas_call(functools.partial(advect_kernel, rows, nfields, lon, chunk...]
where the time goes in v3:
time: 96.8 us; the launch traced here: 96.2 us
  Pallas kernels  96.2 us (99%)
    pallas_call x1, Pallas kernels, per_device(): pl.pallas_call(functools.partial(advect_kernel, rows, nfields, lon, chunk...  91 us
    pallas_call x1, Pallas kernels, per_device(): pl.pallas_call(functools.partial(turn_kernel, nfields, lon), grid=(rows /...  5.19 us

profile of v3, /device:TPU:1, one launch (start us, length us, event | category | flops | bytes accessed | tf_op | source)
XLA Modules:
  0.0 96.2 jit_solution(4246554984461704274)
XLA Ops:
  0.0 91.0 %shard_map.64 = (f32[10,3,8,2560]{3,2,1,0:T(8,128)}, f32[4,128]{1,0:T(4,128)}) custom-call(f32[1,10]{1,0:T(1,128)} %bitcast.3, f32[1,10]{1,0:T(1,128)} %bitcast.4, s32[1,10]{1,0:T(1,128)} %bitcast.5, s32[1,2]{1,0:T(1,128)} %refs_3_.1, f32[10,3,8,2560]{3,2,1,0:T(8,128)} %refs_4_.1), custom_call_target="tpu_custom_call" | custom-call | tf_op jit(solution)/shard_map/pallas_call | solution.py:473
  91.0 5.2 %shard_map.65 = f32[10,3,8,2560]{3,2,1,0:T(8,128)} custom-call(s32[10]{0:T(128)} %shift_ref.1, f32[4,128]{1,0:T(4,128)} %get-tuple-element.7.ratio_ref, f32[10,3,8,2560]{3,2,1,0:T(8,128)} %get-tuple-element.8.column_ref), custom_call_target="tpu_custom_call" | custom-call | tf_op jit(solution)/shard_map/pallas_call | solution.py:485

commit v4 on v3

--- a/solution.py
+++ b/solution.py
@@ -12,6 +12,7 @@
 NY, NZ, NX = 4, 8, 4
 LANES = 128
 ROWS_PER_STEP = 2
+KERNEL_VMEM = 50 * 1024 * 1024
 CHUNKS = [('ring', 1, 1, 1, 2), ('pair', 2, 1, 1, 2), ('pair', 0, 1, 1, 2), ('column', 0, 0, 1, 2), ('column', 2, 0, 1, 2), ('column', 1, 0, 1, 2)]
 ORDER = [0, 3, 2, 5, 3, 0, 4, 5, 2, 1, 3, 4, 5, 0, 2, 1, 4, 3, 2, 0, 1, 4, 5, 1]
 MASS_AT = [2, 8, 15, 16, 23]
@@ -41,15 +42,15 @@
 
 def advect_kernel(rows, nfields, lon, chunks, *refs):
     refs = list(refs)
-    lat_ref, lon_ref, departure_ref, extents_ref, fields_ref, out_ref, ratio_ref = refs[:7]
-    scratch = refs[7:]
+    fractions_ref, numbers_ref, fields_ref, out_ref, ratio_ref = refs[:5]
+    scratch = refs[5:]
     count = len(chunks)
     bufs = []
     for chunk in chunks:
         n = len(buffers_of(chunk[0], rows, 8, LANES))
         bufs.append(scratch[:n])
         scratch = scratch[n:]
-    (out_buf, sums, itab_all, ftab_all, itab, ftab, mass,
+    (sums, itab_all, ftab_all, itab, ftab, mass,
      load_sem, bulk_send, bulk_recv, tab_send, tab_recv, tab_local,
      sum_send, sum_recv, mass_send, mass_recv, out_sem) = scratch
 
@@ -97,12 +98,12 @@
         pl.semaphore_signal(barrier, inc=1, device_id=partner, device_id_type=MESH)
 
     first_row = band * rows
-    low = first_row - extents_ref[0:1, 0:1] * rows + 1
-    high = first_row + rows - 3 + extents_ref[0:1, 1:2] * rows
-    start = jnp.minimum(jnp.maximum(departure_ref[...], low), high)
+    low = first_row - numbers_ref[0:1, rows:rows + 1] * rows + 1
+    high = first_row + rows - 3 + numbers_ref[0:1, rows + 1:rows + 2] * rows
+    start = jnp.minimum(jnp.maximum(numbers_ref[0:1, 0:rows], low), high)
     start = jnp.minimum(jnp.maximum(start, 1), bands * rows - 3) - 1
-    lat_w = cubic_weights(lat_ref[...])
-    lon_w = cubic_weights(lon_ref[...])
+    lat_w = cubic_weights(fractions_ref[0:1])
+    lon_w = cubic_weights(fractions_ref[1:2])
     row_ids = first_row + lax.broadcasted_iota(jnp.int32, (1, rows), 1)
     area = jnp.cos(math.pi * (row_ids.astype(jnp.float32) + 0.5) / (bands * rows) - math.pi / 2.0)
     lon_total = lon_w[0] + lon_w[1] + lon_w[2] + lon_w[3]
@@ -370,7 +371,6 @@
             total = jnp.sum(total, axis=1, keepdims=True)
             ratio_ref[0:4] = jnp.broadcast_to(total[0:4] / total[4:8], (4, LANES))
 
-    outs = [pltpu.make_async_copy(out_buf.at[f], out_ref.at[:, f], out_sem.at[f]) for f in range(nfields)]
 
     def finish(c):
         _, f, lane, width = chunks[c]
@@ -380,22 +380,22 @@
             acc = weighted(src, taps(spot_of, 0, r))
             for extra in extras:
                 acc = acc + extra[r]
-            out_buf[f, r, :, lane:lane + width] = acc
+            out_ref[r, f, :, lane:lane + width] = acc
             return carry
 
         lax.fori_loop(0, rows, one, 0)
 
     def filter_rows(f):
-        def one(r, carry):
-            column = out_buf[f, r]
-            mixed = ftab[0, 5, r] * column
-            for k in range(1, 4):
-                mixed = mixed + ftab[0, 5 + k, r] * pltpu.roll(column, lon - k, 1)
-            out_buf[f, r] = mixed
+        def one(i, carry):
+            for r in (2 * i, 2 * i + 1):
+                column = out_ref[r, f]
+                mixed = ftab[0, 5, r] * column
+                for k in range(1, 4):
+                    mixed = mixed + ftab[0, 5 + k, r] * pltpu.roll(column, lon - k, 1)
+                out_ref[r, f] = mixed
             return carry
 
-        lax.fori_loop(0, rows, one, 0)
-        outs[f].start()
+        lax.fori_loop(0, rows // 2, one, 0)
 
     every = [stages_of(c) for c in range(count)]
     place = [0] * count
@@ -422,8 +422,6 @@
     for group in mass_copies:
         for copy in group:
             copy.wait_send()
-    for copy in outs:
-        copy.wait()
 
 
 def turn_kernel(nfields, lon, shift_ref, ratio_ref, column_ref, out_ref):
@@ -444,7 +442,7 @@
             spots.append(pl.multiple_of(spot * LANES, LANES))
         for f in range(nfields):
             ratio = jnp.broadcast_to(ratio_ref[f:f + 1, :], (8, LANES))
-            turned = [pltpu.roll(column_ref[i, f, :, pl.ds(spot, LANES)], turn, 1) for spot in spots]
+            turned = [pltpu.roll(column_ref[r, f, :, pl.ds(spot, LANES)], turn, 1) for spot in spots]
             for t in range(tiles):
                 out_ref[i, f, :, t * LANES:(t + 1) * LANES] = jnp.where(keep, turned[t], turned[t + 1]) * ratio
 
@@ -459,7 +457,6 @@
     for scheme, _, _, width in chunks:
         scratch += buffers_of(scheme, rows, levels, width)
     scratch += [
-        pltpu.VMEM((nfields, rows, levels, lon), jnp.float32),
         pltpu.VMEM((NY * rows, 8, LANES), jnp.float32),
         pltpu.VMEM((7, 8, LANES), jnp.int32),
         pltpu.VMEM((7, 16, LANES), jnp.float32),
@@ -476,18 +473,19 @@
             jax.ShapeDtypeStruct(fields.shape, fields.dtype),
             jax.ShapeDtypeStruct((4, LANES), jnp.float32),
         ),
-        in_specs=[vmem, vmem, vmem, vmem, pl.BlockSpec(memory_space=pl.ANY)],
-        out_specs=(pl.BlockSpec(memory_space=pl.ANY), vmem),
+        in_specs=[vmem, vmem, pl.BlockSpec(memory_space=pl.ANY)],
+        out_specs=(vmem, vmem),
         scratch_shapes=scratch,
-        compiler_params=pltpu.CompilerParams(collective_id=0, has_side_effects=True),
-    )(lat_fraction[None], lon_fraction[None], departure_row[None], extents, fields)
+        compiler_params=pltpu.CompilerParams(collective_id=0, has_side_effects=True, vmem_limit_bytes=KERNEL_VMEM),
+    )(jnp.stack([lat_fraction, lon_fraction]), jnp.concatenate([departure_row[None], extents], axis=1), fields)
     block = pl.BlockSpec((ROWS_PER_STEP, nfields, levels, lon), lambda i: (i, 0, 0, 0))
     return pl.pallas_call(
         functools.partial(turn_kernel, nfields, lon),
         grid=(rows // ROWS_PER_STEP,),
         out_shape=jax.ShapeDtypeStruct(fields.shape, fields.dtype),
-        in_specs=[pl.BlockSpec(memory_space=pltpu.SMEM), vmem, block],
+        in_specs=[pl.BlockSpec(memory_space=pltpu.SMEM), vmem, vmem],
         out_specs=block,
+        compiler_params=pltpu.CompilerParams(vmem_limit_bytes=16 * 1024 * 1024),
     )(lon_shift, ratio, column)
 
 

time: 96.8 us -> 94.2 us (0.973)
  Pallas kernels: 96.2 us -> 92.3 us
  other arithmetic: 0 us -> 1.44 us
    pallas_call x1, Pallas kernels: 91 us -> 88.7 us  [per_device(): pl.pallas_call(functools.partial(advect_kernel, rows, nfields, lon, chunk...]
    pallas_call x1, Pallas kernels: 5.19 us -> 3.65 us  [per_device(): pl.pallas_call(functools.partial(turn_kernel, nfields, lon), grid=(rows /...]
where the time goes in v4:
time: 94.2 us; the launch traced here: 93.8 us
  Pallas kernels  92.3 us (98%)
  other arithmetic  1.44 us (2%)
    pallas_call x1, Pallas kernels, per_device(): pl.pallas_call(functools.partial(advect_kernel, rows, nfields, lon, chunk...  88.7 us
    pallas_call x1, Pallas kernels, per_device(): pl.pallas_call(functools.partial(turn_kernel, nfields, lon), grid=(rows /...  3.65 us

profile of v4, /device:TPU:1, one launch (start us, length us, event | category | flops | bytes accessed | tf_op | source)
XLA Modules:
  0.0 93.8 jit_solution(9400585921424138194)
XLA Ops:
  0.0 0.0 copy-start
  0.0 0.8 pad_add_fusion.refs_1_
  0.8 0.7 pad_maximum_fusion.refs_0_
  1.4 88.7 %shard_map.64 = (f32[10,3,8,2560]{3,2,1,0:T(8,128)S(1)}, f32[4,128]{1,0:T(4,128)S(1)}) custom-call(f32[2,10]{1,0:T(2,128)S(1)} %pad_maximum_fusion.refs_0_, s32[1,12]{1,0:T(1,128)S(1)} %pad_add_fusion.refs_1_, f32[10,3,8,2560]{3,2,1,0:T(8,128)} %refs_2_.1), custom_call_target="tpu_custom_call" | custom-call | tf_op jit(solution)/shard_map/pallas_call | solution.py:470
  90.1 0.0 copy-done
  90.1 3.6 %shard_map.65 = f32[10,3,8,2560]{3,2,1,0:T(8,128)} custom-call(s32[10]{0:T(128)S(1)} %copy-done, f32[4,128]{1,0:T(4,128)S(1)} %get-tuple-element.7.ratio_ref, f32[10,3,8,2560]{3,2,1,0:T(8,128)S(1)} %get-tuple-element.8.column_ref), custom_call_target="tpu_custom_call" | custom-call | tf_op jit(solution)/shard_map/pallas_call | solution.py:482
Async XLA Ops:
  0.0 90.1 %copy-start = (s32[10]{0:T(128)S(1)}, s32[10]{0:T(128)}, u32[]{:S(2)}) copy-start(s32[10]{0:T(128)} %shift_ref.1) | copy-start | bytes 124

commit v5 on v4

--- a/solution.py
+++ b/solution.py
@@ -13,9 +13,9 @@
 LANES = 128
 ROWS_PER_STEP = 2
 KERNEL_VMEM = 50 * 1024 * 1024
-CHUNKS = [('ring', 1, 1, 1, 2), ('pair', 2, 1, 1, 2), ('pair', 0, 1, 1, 2), ('column', 0, 0, 1, 2), ('column', 2, 0, 1, 2), ('column', 1, 0, 1, 2)]
-ORDER = [0, 3, 2, 5, 3, 0, 4, 5, 2, 1, 3, 4, 5, 0, 2, 1, 4, 3, 2, 0, 1, 4, 5, 1]
-MASS_AT = [2, 8, 15, 16, 23]
+CHUNKS = [('pair', 0, 0, 5), ('mirror', 0, 5, 5), ('pair', 0, 10, 10), ('ring', 1, 0, 15), ('column', 1, 15, 5), ('mirror', 2, 0, 10), ('ring', 2, 10, 5), ('column', 2, 15, 5)]
+ORDER = [4, 0, 1, 2, 5, 7, 1, 3, 0, 1, 5, 6, 2, 0, 3, 4, 7, 2, 6, 5, 4, 0, 3, 6, 2, 7, 3, 5, 1, 4, 6, 7]
+MASS_AT = [3, 11, 24, 25, 31]
 
 
 def cubic_weights(fraction):
@@ -33,11 +33,26 @@
         "ring": [NY * rows] + [rows] * 4,
         "column": [3 * rows] + [rows] * 3 + [half, rows - half] + [rows] * 2,
         "pair": [2 * rows] + [rows] * 8,
+        "mirror": [2 * rows] + [rows] * 8,
     }[scheme]
     return [pltpu.VMEM((n, levels, width), jnp.float32) for n in counts]
 
 
-COPIES = {"ring": 6, "column": 6, "pair": 5}
+COPIES = {"ring": 6, "column": 6, "pair": 5, "mirror": 5}
+
+
+class Guarded:
+    def __init__(self, copy, sends, gets):
+        self.copy, self.sends, self.gets = copy, sends, gets
+
+    def start(self):
+        pl.when(self.sends)(lambda: self.copy.start())
+
+    def wait_recv(self):
+        pl.when(self.gets)(lambda: self.copy.wait_recv())
+
+    def wait_send(self):
+        pl.when(self.sends)(lambda: self.copy.wait_send())
 
 
 def advect_kernel(rows, nfields, lon, chunks, *refs):
@@ -75,9 +90,15 @@
     cross = (base + 3 - y, core)
     toward = (lax.rem(band + bands - NY + 2 * NY * south, bands), core)
     diagonal = (lax.rem(base + 3 - y + bands - NY + 2 * NY * south, bands), core)
-    partners = y_mates + z_mates + x_mates + c_mates + [up, down, diagonal]
-
-    own_at = {"ring": y * rows, "column": rows, "pair": odd * rows}
+    outer = jnp.logical_or(y == 0, y == NY - 1)
+    inner = jnp.logical_not(outer)
+    toward_main = (lax.rem(band + NY + bands - 2 * NY * south, bands), core)
+    behind = toward
+    before = (lax.rem(band + 1 - 2 * odd + NY + bands - 2 * NY * south, bands), core)
+    after = (lax.rem(band + 1 - 2 * odd + bands - NY + 2 * NY * south, bands), core)
+    partners = y_mates + z_mates + x_mates + c_mates + [up, down, diagonal, before, after]
+
+    own_at = {"ring": y * rows, "column": rows, "pair": odd * rows, "mirror": south * rows}
     loads = [
         pltpu.make_async_copy(
             fields_ref.at[:, f, :, pl.ds(lane, width)],
@@ -93,9 +114,39 @@
     for c in loaded_first:
         loads[c].start()
 
+    can_up, can_down = band + NY < bands, band >= NY
+    by_half = lambda north, south_side: jnp.logical_or(
+        jnp.logical_and(south == 0, north), jnp.logical_and(south == 1, south_side)
+    )
+    to_up_down, to_down_up = by_half(can_up, can_down), by_half(can_down, can_up)
+
     barrier = pltpu.get_barrier_semaphore()
     for partner in partners:
         pl.semaphore_signal(barrier, inc=1, device_id=partner, device_id_type=MESH)
+
+    def clear(ref, first, n):
+        def one(r, carry):
+            ref[first + r] = jnp.zeros(ref.shape[1:], jnp.float32)
+            return carry
+
+        lax.fori_loop(0, n, one, 0)
+
+    for at_end, side in ((jnp.logical_not(can_down), 0), (jnp.logical_not(can_up), 1)):
+
+        @pl.when(at_end)
+        def _(side=side):
+            for b, chunk in zip(bufs, chunks):
+                if chunk[0] == "ring":
+                    clear(b[3 + side], 0, rows)
+                elif chunk[0] == "column":
+                    clear(b[0], 2 * side * rows, rows)
+                elif chunk[0] == "pair":
+                    clear(b[5 + side], 0, rows)
+                    pl.when(south == 1 - side)(lambda b=b: clear(b[7], 0, rows))
+                else:
+                    pl.when(south == side)(lambda b=b: clear(b[5], 0, rows))
+                    pl.when(south == side)(lambda b=b: clear(b[7], 0, rows))
+                    pl.when(south == 1 - side)(lambda b=b: clear(b[6], 0, rows))
 
     first_row = band * rows
     low = first_row - numbers_ref[0:1, rows:rows + 1] * rows + 1
@@ -140,7 +191,7 @@
             src_ref=src, dst_ref=dst, send_sem=send_sem, recv_sem=recv_sem, device_id=target, device_id_type=MESH
         )
 
-    table_routes = [(2, up), (1, down), (5, y_mates[0]), (4, y_mates[1]), (3, y_mates[2]), (6, diagonal)]
+    table_routes = [(2, up), (1, down), (5, y_mates[0]), (4, y_mates[1]), (3, y_mates[2]), (6, diagonal), (7, after)]
     tables = []
     for i, (slot, target) in enumerate(table_routes):
         for j, ref in enumerate((itab_all, ftab_all)):
@@ -159,6 +210,21 @@
     def pair_spot(row):
         spot = row - (band - odd) * rows
         return jnp.clip(spot, 0, 2 * rows - 1), jnp.logical_and(spot >= 0, spot < 2 * rows)
+
+    mirror_low = (base + jnp.where(outer, 0, 1)) * rows
+    mirror_high = (base + jnp.where(outer, 3, 2)) * rows
+    mirror_far = (band + NY - 2 * NY * south) * rows
+
+    def mirror_spot(row):
+        low_at, high_at = row - mirror_low, row - mirror_high
+        in_low = jnp.logical_and(low_at >= 0, low_at < rows)
+        in_high = jnp.logical_and(high_at >= 0, high_at < rows)
+        spot = jnp.where(in_low, low_at, jnp.clip(high_at, 0, rows - 1) + rows)
+        return spot, jnp.logical_or(in_low, in_high)
+
+    def far_spot(row):
+        away = row - mirror_far
+        return jnp.clip(away, 0, rows - 1), jnp.logical_and(away >= 0, away < rows)
 
     def column_spot(row):
         away = row - (band - NY) * rows
@@ -224,7 +290,16 @@
         recv = [bulk_recv.at[c, k] for k in range(COPIES[scheme])]
 
         def link(k, src, dst, target):
-            return remote(src, dst, send[k], recv[k], target)
+            copy = remote(src, dst, send[k], recv[k], target)
+            if target is up:
+                return Guarded(copy, can_up, can_down)
+            if target is down:
+                return Guarded(copy, can_down, can_up)
+            if target is toward:
+                return Guarded(copy, to_down_up, to_up_down)
+            if target is toward_main:
+                return Guarded(copy, to_up_down, to_down_up)
+            return copy
 
         if scheme == "ring":
             ring, send_up, send_down, recv_up, recv_down = b
@@ -258,7 +333,7 @@
             def stage3():
                 copies[4].wait_recv()
                 copies[5].wait_recv()
-                finals[c] = (ring_spot, ring, [recv_up, recv_down])
+                finals[c] = (ring_spot, ring, [recv_up, recv_down], None)
 
         elif scheme == "column":
             column, to_up, to_down, to_far, far_a, far_b, got_a, got_b = b
@@ -294,7 +369,56 @@
             def stage3():
                 copies[4].wait_recv()
                 copies[5].wait_recv()
-                finals[c] = (column_spot, column, [got_a, got_b])
+                finals[c] = (column_spot, column, [got_a, got_b], None)
+
+        elif scheme == "mirror":
+            both, to_main, to_behind, to_far, to_cross, from_main, from_behind, passed, from_cross = b
+            mine = both.at[pl.ds(south * rows, rows)]
+            copies = [
+                link(0, mine, mine, cross), link(1, to_main, from_main, toward_main),
+                link(2, to_behind, from_behind, behind), link(3, to_far, passed, toward_main),
+                link(4, to_cross, from_cross, pair),
+            ]
+            raw = link(2, mine, from_behind, behind)
+
+            def stage0():
+                copies[0].start()
+                pl.when(outer)(lambda: raw.start())
+
+            def stage1():
+                copies[0].wait_recv()
+                need_tables()
+                partial_rows(mirror_spot, both, [(7, to_far, None)])
+                copies[3].start()
+                partial_rows(mirror_spot, both, [(1 + south, to_main, None)])
+                copies[1].start()
+
+                @pl.when(inner)
+                def _():
+                    partial_rows(mirror_spot, both, [(2 - south, to_behind, None)])
+                    copies[2].start()
+
+            def stage2():
+                copies[3].wait_recv()
+                partial_rows(mirror_spot, both, [(3 + 2 * odd, to_cross, passed)])
+
+                @pl.when(outer)
+                def _():
+                    copies[2].wait_recv()
+
+                    def one(r, carry):
+                        to_cross[r] = to_cross[r] + weighted(from_behind, taps(far_spot, 3 + 2 * odd, r))
+                        return carry
+
+                    lax.fori_loop(0, rows, one, 0)
+
+                copies[4].start()
+
+            def stage3():
+                copies[1].wait_recv()
+                copies[4].wait_recv()
+                pl.when(inner)(lambda: copies[2].wait_recv())
+                finals[c] = (mirror_spot, both, [from_main, from_cross], from_behind)
 
         else:
             both, to_up, to_down, to_diag, to_cross, from_down, from_up, passed, from_cross = b
@@ -325,7 +449,7 @@
                 copies[1].wait_recv()
                 copies[2].wait_recv()
                 copies[4].wait_recv()
-                finals[c] = (pair_spot, both, [from_down, from_up, from_cross])
+                finals[c] = (pair_spot, both, [from_down, from_up, from_cross], None)
 
         return copies, [stage0, stage1, stage2, stage3]
 
@@ -374,7 +498,7 @@
 
     def finish(c):
         _, f, lane, width = chunks[c]
-        spot_of, src, extras = finals[c]
+        spot_of, src, extras, far = finals[c]
 
         def one(r, carry):
             acc = weighted(src, taps(spot_of, 0, r))
@@ -384,6 +508,25 @@
             return carry
 
         lax.fori_loop(0, rows, one, 0)
+        if far is None:
+            return
+
+        @pl.when(inner)
+        def _():
+            def more(r, carry):
+                out_ref[r, f, :, lane:lane + width] = out_ref[r, f, :, lane:lane + width] + far[r]
+                return carry
+
+            lax.fori_loop(0, rows, more, 0)
+
+        @pl.when(outer)
+        def _():
+            def more(r, carry):
+                acc = weighted(far, taps(far_spot, 0, r))
+                out_ref[r, f, :, lane:lane + width] = out_ref[r, f, :, lane:lane + width] + acc
+                return carry
+
+            lax.fori_loop(0, rows, more, 0)
 
     def filter_rows(f):
         def one(i, carry):
@@ -449,7 +592,7 @@
 
 def per_device(fields, lat_fraction, lon_fraction, lon_shift, departure_row, extents):
     rows, nfields, levels, lon = fields.shape
-    chunks = [(k, f, lon * lane // parts, lon * width // parts) for k, f, lane, width, parts in CHUNKS]
+    chunks = [(k, f, lane * LANES, width * LANES) for k, f, lane, width in CHUNKS]
     count = len(chunks)
     dma = pltpu.SemaphoreType.DMA
     mates = (NX - 1) + 1 + (NZ - 1) + (NY - 1)
@@ -458,12 +601,12 @@
         scratch += buffers_of(scheme, rows, levels, width)
     scratch += [
         pltpu.VMEM((NY * rows, 8, LANES), jnp.float32),
-        pltpu.VMEM((7, 8, LANES), jnp.int32),
-        pltpu.VMEM((7, 16, LANES), jnp.float32),
-        pltpu.SMEM((7, 8, LANES), jnp.int32),
-        pltpu.SMEM((7, 16, LANES), jnp.float32),
+        pltpu.VMEM((8, 8, LANES), jnp.int32),
+        pltpu.VMEM((8, 16, LANES), jnp.float32),
+        pltpu.SMEM((8, 8, LANES), jnp.int32),
+        pltpu.SMEM((8, 16, LANES), jnp.float32),
         pltpu.VMEM((4 + mates, 8, LANES), jnp.float32),
-        dma((count,)), dma((count, 6)), dma((count, 6)), dma((12,)), dma((12,)), dma((2,)),
+        dma((count,)), dma((count, 6)), dma((count, 6)), dma((14,)), dma((14,)), dma((2,)),
         dma((NY - 1,)), dma((NY - 1,)), dma((mates,)), dma((mates,)), dma((nfields,)),
     ]
     vmem = pl.BlockSpec(memory_space=pltpu.VMEM)

time: 94.2 us -> 90.4 us (0.960)
  Pallas kernels: 92.3 us -> 88.5 us
    pallas_call x1, Pallas kernels: 88.7 us -> 84.9 us  [per_device(): pl.pallas_call(functools.partial(advect_kernel, rows, nfields, lon, chunk...]
where the time goes in v5:
time: 90.4 us; the launch traced here: 90 us
  Pallas kernels  88.5 us (98%)
  other arithmetic  1.44 us (2%)
    pallas_call x1, Pallas kernels, per_device(): pl.pallas_call(functools.partial(advect_kernel, rows, nfields, lon, chunk...  84.9 us
    pallas_call x1, Pallas kernels, per_device(): pl.pallas_call(functools.partial(turn_kernel, nfields, lon), grid=(rows /...  3.65 us

profile of v5, /device:TPU:1, one launch (start us, length us, event | category | flops | bytes accessed | tf_op | source)
XLA Modules:
  0.0 90.0 jit_solution(17324728941764628872)
XLA Ops:
  0.0 0.0 copy-start
  0.0 0.8 pad_add_fusion.refs_1_
  0.8 0.7 pad_maximum_fusion.refs_0_
  1.4 84.9 %shard_map.64 = (f32[10,3,8,2560]{3,2,1,0:T(8,128)S(1)}, f32[4,128]{1,0:T(4,128)S(1)}) custom-call(f32[2,10]{1,0:T(2,128)S(1)} %pad_maximum_fusion.refs_0_, s32[1,12]{1,0:T(1,128)S(1)} %pad_add_fusion.refs_1_, f32[10,3,8,2560]{3,2,1,0:T(8,128)} %refs_2_.1), custom_call_target="tpu_custom_call" | custom-call | tf_op jit(solution)/shard_map/pallas_call | solution.py:613
  86.3 0.0 copy-done
  86.3 3.6 %shard_map.65 = f32[10,3,8,2560]{3,2,1,0:T(8,128)} custom-call(s32[10]{0:T(128)S(1)} %copy-done, f32[4,128]{1,0:T(4,128)S(1)} %get-tuple-element.7.ratio_ref, f32[10,3,8,2560]{3,2,1,0:T(8,128)S(1)} %get-tuple-element.8.column_ref), custom_call_target="tpu_custom_call" | custom-call | tf_op jit(solution)/shard_map/pallas_call | solution.py:625
Async XLA Ops:
  0.0 86.3 %copy-start = (s32[10]{0:T(128)S(1)}, s32[10]{0:T(128)}, u32[]{:S(2)}) copy-start(s32[10]{0:T(128)} %shift_ref.1) | copy-start | bytes 124

commit v6 on v5

--- a/solution.py
+++ b/solution.py
@@ -11,11 +11,12 @@
 MESH = pl.DeviceIdType.MESH
 NY, NZ, NX = 4, 8, 4
 LANES = 128
-ROWS_PER_STEP = 2
+ROWS_PER_STEP = 5
+UNROLL = 2
 KERNEL_VMEM = 50 * 1024 * 1024
-CHUNKS = [('pair', 0, 0, 5), ('mirror', 0, 5, 5), ('pair', 0, 10, 10), ('ring', 1, 0, 15), ('column', 1, 15, 5), ('mirror', 2, 0, 10), ('ring', 2, 10, 5), ('column', 2, 15, 5)]
-ORDER = [4, 0, 1, 2, 5, 7, 1, 3, 0, 1, 5, 6, 2, 0, 3, 4, 7, 2, 6, 5, 4, 0, 3, 6, 2, 7, 3, 5, 1, 4, 6, 7]
-MASS_AT = [3, 11, 24, 25, 31]
+CHUNKS = [('column', 0, 0, 10), ('mirror', 0, 10, 10), ('ring', 1, 0, 15), ('column', 1, 15, 5), ('mirror', 2, 0, 5), ('pair', 2, 5, 15)]
+ORDER = [0, 4, 5, 1, 2, 3, 4, 0, 5, 1, 2, 0, 3, 5, 1, 2, 0, 4, 3, 1, 4, 5, 2, 3]
+MASS_AT = [2, 8, 18, 18, 23]
 
 
 def cubic_weights(fraction):
@@ -247,14 +248,21 @@
             acc = term if acc is None else acc + term
         return acc
 
+    def each_row(one):
+        def several(i, carry):
+            for k in range(UNROLL):
+                one(UNROLL * i + k)
+            return carry
+
+        lax.fori_loop(0, rows // UNROLL, several, 0)
+
     def partial_rows(spot_of, src, jobs):
-        def one(r, carry):
+        def one(r):
             for t, dst, extra in jobs:
                 acc = weighted(src, taps(spot_of, t, r))
                 dst[r] = acc if extra is None else acc + extra[r]
-            return carry
-
-        lax.fori_loop(0, rows, one, 0)
+
+        each_row(one)
 
     def add_rows(n, dst, dst_at, extra):
         def one(r, carry):
@@ -500,14 +508,13 @@
         _, f, lane, width = chunks[c]
         spot_of, src, extras, far = finals[c]
 
-        def one(r, carry):
+        def one(r):
             acc = weighted(src, taps(spot_of, 0, r))
             for extra in extras:
                 acc = acc + extra[r]
             out_ref[r, f, :, lane:lane + width] = acc
-            return carry
-
-        lax.fori_loop(0, rows, one, 0)
+
+        each_row(one)
         if far is None:
             return
 
@@ -529,16 +536,14 @@
             lax.fori_loop(0, rows, more, 0)
 
     def filter_rows(f):
-        def one(i, carry):
-            for r in (2 * i, 2 * i + 1):
-                column = out_ref[r, f]
-                mixed = ftab[0, 5, r] * column
-                for k in range(1, 4):
-                    mixed = mixed + ftab[0, 5 + k, r] * pltpu.roll(column, lon - k, 1)
-                out_ref[r, f] = mixed
-            return carry
-
-        lax.fori_loop(0, rows // 2, one, 0)
+        def one(r):
+            column = out_ref[r, f]
+            mixed = ftab[0, 5, r] * column
+            for k in range(1, 4):
+                mixed = mixed + ftab[0, 5 + k, r] * pltpu.roll(column, lon - k, 1)
+            out_ref[r, f] = mixed
+
+        each_row(one)
 
     every = [stages_of(c) for c in range(count)]
     place = [0] * count

time: 90.4 us -> 87.2 us (0.965)
  Pallas kernels: 88.5 us -> 85.6 us
    pallas_call x1, Pallas kernels: 84.9 us -> 83.1 us  [per_device(): pl.pallas_call(functools.partial(advect_kernel, rows, nfields, lon, chunk...]
    pallas_call x1, Pallas kernels: 3.65 us -> 2.52 us  [per_device(): pl.pallas_call(functools.partial(turn_kernel, nfields, lon), grid=(rows /...]
where the time goes in v6:
time: 87.2 us; the launch traced here: 87.1 us
  Pallas kernels  85.6 us (98%)
  other arithmetic  1.44 us (2%)
    pallas_call x1, Pallas kernels, per_device(): pl.pallas_call(functools.partial(advect_kernel, rows, nfields, lon, chunk...  83.1 us
    pallas_call x1, Pallas kernels, per_device(): pl.pallas_call(functools.partial(turn_kernel, nfields, lon), grid=(rows /...  2.52 us

profile of v6, /device:TPU:1, one launch (start us, length us, event | category | flops | bytes accessed | tf_op | source)
XLA Modules:
  0.0 87.1 jit_solution(1667117584451912419)
XLA Ops:
  0.0 0.0 copy-start
  0.0 0.8 pad_add_fusion.refs_1_
  0.8 0.7 pad_maximum_fusion.refs_0_
  1.4 83.1 %shard_map.64 = (f32[10,3,8,2560]{3,2,1,0:T(8,128)S(1)}, f32[4,128]{1,0:T(4,128)S(1)}) custom-call(f32[2,10]{1,0:T(2,128)S(1)} %pad_maximum_fusion.refs_0_, s32[1,12]{1,0:T(1,128)S(1)} %pad_add_fusion.refs_1_, f32[10,3,8,2560]{3,2,1,0:T(8,128)} %refs_2_.1), custom_call_target="tpu_custom_call" | custom-call | tf_op jit(solution)/shard_map/pallas_call | solution.py:618
  84.5 0.0 copy-done
  84.6 2.5 %shard_map.65 = f32[10,3,8,2560]{3,2,1,0:T(8,128)} custom-call(s32[10]{0:T(128)S(1)} %copy-done, f32[4,128]{1,0:T(4,128)S(1)} %get-tuple-element.7.ratio_ref, f32[10,3,8,2560]{3,2,1,0:T(8,128)S(1)} %get-tuple-element.8.column_ref), custom_call_target="tpu_custom_call" | custom-call | tf_op jit(solution)/shard_map/pallas_call | solution.py:630
Async XLA Ops:
  0.0 84.5 %copy-start = (s32[10]{0:T(128)S(1)}, s32[10]{0:T(128)}, u32[]{:S(2)}) copy-start(s32[10]{0:T(128)} %shift_ref.1) | copy-start | bytes 124

commit v7 on v6

--- a/solution.py
+++ b/solution.py
@@ -11,7 +11,7 @@
 MESH = pl.DeviceIdType.MESH
 NY, NZ, NX = 4, 8, 4
 LANES = 128
-ROWS_PER_STEP = 5
+ROWS_PER_STEP = 1
 UNROLL = 2
 KERNEL_VMEM = 50 * 1024 * 1024
 CHUNKS = [('column', 0, 0, 10), ('mirror', 0, 10, 10), ('ring', 1, 0, 15), ('column', 1, 15, 5), ('mirror', 2, 0, 5), ('pair', 2, 5, 15)]
@@ -572,27 +572,32 @@
             copy.wait_send()
 
 
-def turn_kernel(nfields, lon, shift_ref, ratio_ref, column_ref, out_ref):
+def turn_kernel(rows, nfields, lon, shift_ref, ratio_ref, column_ref, out_ref, turned_buf, out_sem):
     lane_id = lax.broadcasted_iota(jnp.int32, (8, LANES), 1)
     tiles = lon // LANES
-    for i in range(ROWS_PER_STEP):
-        r = pl.program_id(0) * ROWS_PER_STEP + i
-        begin = shift_ref[r] - 1
-        begin = jnp.where(begin < 0, begin + lon, begin)
-        whole = lax.shift_right_logical(begin, 7)
-        rest = jnp.bitwise_and(begin, LANES - 1)
-        turn = jnp.bitwise_and(LANES - rest, LANES - 1)
-        keep = lane_id < (LANES - rest)
-        spots = []
-        for t in range(tiles + 1):
-            spot = whole + t
-            spot = jnp.where(spot >= tiles, spot - tiles, spot)
-            spots.append(pl.multiple_of(spot * LANES, LANES))
-        for f in range(nfields):
-            ratio = jnp.broadcast_to(ratio_ref[f:f + 1, :], (8, LANES))
-            turned = [pltpu.roll(column_ref[r, f, :, pl.ds(spot, LANES)], turn, 1) for spot in spots]
-            for t in range(tiles):
-                out_ref[i, f, :, t * LANES:(t + 1) * LANES] = jnp.where(keep, turned[t], turned[t + 1]) * ratio
+    copies = []
+    for step in range(rows // ROWS_PER_STEP):
+        at = pl.ds(step * ROWS_PER_STEP, ROWS_PER_STEP)
+        copies.append(pltpu.make_async_copy(turned_buf.at[at], out_ref.at[at], out_sem.at[step]))
+        for r in range(step * ROWS_PER_STEP, (step + 1) * ROWS_PER_STEP):
+            begin = shift_ref[r] - 1
+            begin = jnp.where(begin < 0, begin + lon, begin)
+            whole = lax.shift_right_logical(begin, 7)
+            spots = []
+            for t in range(tiles + 1):
+                spot = whole + t
+                spots.append(pl.multiple_of(jnp.where(spot >= tiles, spot - tiles, spot) * LANES, LANES))
+            rest = jnp.bitwise_and(begin, LANES - 1)
+            turn = jnp.bitwise_and(LANES - rest, LANES - 1)
+            keep = lane_id < (LANES - rest)
+            for f in range(nfields):
+                ratio = jnp.broadcast_to(ratio_ref[f:f + 1, :], (8, LANES))
+                turned = [pltpu.roll(column_ref[r, f, :, pl.ds(spot, LANES)], turn, 1) for spot in spots]
+                for t in range(tiles):
+                    turned_buf[r, f, :, t * LANES:(t + 1) * LANES] = jnp.where(keep, turned[t], turned[t + 1]) * ratio
+        copies[-1].start()
+    for copy in copies:
+        copy.wait()
 
 
 def per_device(fields, lat_fraction, lon_fraction, lon_shift, departure_row, extents):
@@ -626,13 +631,12 @@
         scratch_shapes=scratch,
         compiler_params=pltpu.CompilerParams(collective_id=0, has_side_effects=True, vmem_limit_bytes=KERNEL_VMEM),
     )(jnp.stack([lat_fraction, lon_fraction]), jnp.concatenate([departure_row[None], extents], axis=1), fields)
-    block = pl.BlockSpec((ROWS_PER_STEP, nfields, levels, lon), lambda i: (i, 0, 0, 0))
     return pl.pallas_call(
-        functools.partial(turn_kernel, nfields, lon),
-        grid=(rows // ROWS_PER_STEP,),
+        functools.partial(turn_kernel, rows, nfields, lon),
         out_shape=jax.ShapeDtypeStruct(fields.shape, fields.dtype),
         in_specs=[pl.BlockSpec(memory_space=pltpu.SMEM), vmem, vmem],
-        out_specs=block,
+        out_specs=pl.BlockSpec(memory_space=pl.ANY),
+        scratch_shapes=[pltpu.VMEM(fields.shape, fields.dtype), dma((rows // ROWS_PER_STEP,))],
         compiler_params=pltpu.CompilerParams(vmem_limit_bytes=16 * 1024 * 1024),
     )(lon_shift, ratio, column)
 

time: 87.2 us -> 86.9 us (level)
  no operation moved by 1% of the time
where the time goes in v7:
time: 86.9 us; the launch traced here: 86.8 us
  Pallas kernels  85.3 us (98%)
  other arithmetic  1.44 us (2%)
    pallas_call x1, Pallas kernels, per_device(): pl.pallas_call(functools.partial(advect_kernel, rows, nfields, lon, chunk...  83.1 us
    pallas_call x1, Pallas kernels, per_device(): pl.pallas_call(functools.partial(turn_kernel, rows, nfields, lon), out_sh...  2.22 us

profile of v7, /device:TPU:1, one launch (start us, length us, event | category | flops | bytes accessed | tf_op | source)
XLA Modules:
  0.0 86.8 jit_solution(15432692014629120049)
XLA Ops:
  0.0 0.0 copy-start
  0.0 0.8 pad_add_fusion.refs_1_
  0.8 0.7 pad_maximum_fusion.refs_0_
  1.4 83.1 %shard_map.64 = (f32[10,3,8,2560]{3,2,1,0:T(8,128)S(1)}, f32[4,128]{1,0:T(4,128)S(1)}) custom-call(f32[2,10]{1,0:T(2,128)S(1)} %pad_maximum_fusion.refs_0_, s32[1,12]{1,0:T(1,128)S(1)} %pad_add_fusion.refs_1_, f32[10,3,8,2560]{3,2,1,0:T(8,128)} %refs_2_.1), custom_call_target="tpu_custom_call" | custom-call | tf_op jit(solution)/shard_map/pallas_call | solution.py:623
  84.5 0.0 copy-done
  84.6 2.2 %shard_map.65 = f32[10,3,8,2560]{3,2,1,0:T(8,128)} custom-call(s32[10]{0:T(128)S(1)} %copy-done, f32[4,128]{1,0:T(4,128)S(1)} %get-tuple-element.7.ratio_ref, f32[10,3,8,2560]{3,2,1,0:T(8,128)S(1)} %get-tuple-element.8.column_ref), custom_call_target="tpu_custom_call" | custom-call | tf_op jit(solution)/shard_map/pallas_call | solution.py:634
Async XLA Ops:
  0.0 84.5 %copy-start = (s32[10]{0:T(128)S(1)}, s32[10]{0:T(128)}, u32[]{:S(2)}) copy-start(s32[10]{0:T(128)} %shift_ref.1) | copy-start | bytes 124

commit v8 on v7

--- a/solution.py
+++ b/solution.py
@@ -165,9 +165,6 @@
     for k, values in enumerate(lat_w + [area * lon_total] + lon_w + [area]):
         ftab_all[0, k:k + 1, 0:rows] = values
 
-    for load in loads:
-        load.wait()
-
     def row_sums(r, carry):
         pieces = []
         for f in range(nfields):
@@ -184,7 +181,6 @@
         sums[y * rows + r] = jnp.concatenate(pieces, axis=0)
         return carry
 
-    lax.fori_loop(0, rows, row_sums, 0)
     pl.semaphore_wait(barrier, len(partners))
 
     def remote(src, dst, send_sem, recv_sem, target):
@@ -201,9 +197,6 @@
         copy.start()
     my_sums = sums.at[pl.ds(y * rows, rows)]
     sum_copies = [remote(my_sums, my_sums, sum_send.at[s], sum_recv.at[s], y_mates[s]) for s in range(NY - 1)]
-    for copy in sum_copies:
-        copy.start()
-
     def ring_spot(row):
         spot = row - base * rows
         return jnp.clip(spot, 0, NY * rows - 1), jnp.logical_and(spot >= 0, spot < NY * rows)
@@ -550,6 +543,15 @@
     left = [sum(1 for chunk in chunks if chunk[1] == f) for f in range(nfields)]
     mass_done = 0
     for i, c in enumerate(ORDER):
+        if i == 0:
+            loads[c].wait()
+        if i == 1:
+            for other in range(count):
+                if other != ORDER[0]:
+                    loads[other].wait()
+            lax.fori_loop(0, rows, row_sums, 0)
+            for copy in sum_copies:
+                copy.start()
         every[c][1][place[c]]()
         place[c] += 1
         if place[c] == 4:

time: 86.9 us -> 87.4 us (level)
  no operation moved by 1% of the time
where the time goes in v8:
time: 87.4 us; the launch traced here: 87.3 us
  Pallas kernels  85.8 us (98%)
  other arithmetic  1.44 us (2%)
    pallas_call x1, Pallas kernels, per_device(): pl.pallas_call(functools.partial(advect_kernel, rows, nfields, lon, chunk...  83.6 us
    pallas_call x1, Pallas kernels, per_device(): pl.pallas_call(functools.partial(turn_kernel, rows, nfields, lon), out_sh...  2.22 us

profile of v8, /device:TPU:1, one launch (start us, length us, event | category | flops | bytes accessed | tf_op | source)
XLA Modules:
  0.0 87.3 jit_solution(4119870878669975377)
XLA Ops:
  0.0 0.0 copy-start
  0.0 0.8 pad_add_fusion.refs_1_
  0.8 0.7 pad_maximum_fusion.refs_0_
  1.4 83.6 %shard_map.64 = (f32[10,3,8,2560]{3,2,1,0:T(8,128)S(1)}, f32[4,128]{1,0:T(4,128)S(1)}) custom-call(f32[2,10]{1,0:T(2,128)S(1)} %pad_maximum_fusion.refs_0_, s32[1,12]{1,0:T(1,128)S(1)} %pad_add_fusion.refs_1_, f32[10,3,8,2560]{3,2,1,0:T(8,128)} %refs_2_.1), custom_call_target="tpu_custom_call" | custom-call | tf_op jit(solution)/shard_map/pallas_call | solution.py:625
  85.1 0.0 copy-done
  85.1 2.2 %shard_map.65 = f32[10,3,8,2560]{3,2,1,0:T(8,128)} custom-call(s32[10]{0:T(128)S(1)} %copy-done, f32[4,128]{1,0:T(4,128)S(1)} %get-tuple-element.7.ratio_ref, f32[10,3,8,2560]{3,2,1,0:T(8,128)S(1)} %get-tuple-element.8.column_ref), custom_call_target="tpu_custom_call" | custom-call | tf_op jit(solution)/shard_map/pallas_call | solution.py:636
Async XLA Ops:
  0.0 85.1 %copy-start = (s32[10]{0:T(128)S(1)}, s32[10]{0:T(128)}, u32[]{:S(2)}) copy-start(s32[10]{0:T(128)} %shift_ref.1) | copy-start | bytes 124
